TPU v7x, 32 devices: a whole 2x2x4 slice. The times are simulated.
32 devices in a mesh: dp: 2 (over x), ch: 4 (over z), wd: 4 (over y, core).
Axes of the slice: x: 2, y: 2, z: 4, core: 2. Of those that a mesh axis runs over, the one named last changes fastest.
Arguments:
- resid_in: bfloat16 [8192, 4096], P('dp', 'wd'), parts along dimension 0
- seg_pos: int32 [2, 4096], P('dp'), parts along dimension 0
- gain_temporal: bfloat16 [4096], P('wd')
- w_x: bfloat16 [4096, 4096], P('wd', 'ch')
- bias_x: bfloat16 [4096], P('ch')
- w_y: bfloat16 [4096, 4096], P('wd', 'ch')
- bias_y: bfloat16 [4096], P('ch')
- conv_w: bfloat16 [4, 4096], P(None, 'ch')
- conv_bias: bfloat16 [4096], P('ch')
- lam_param: float32 [4096], P('ch')
- rgate_w: bfloat16 [16, 256, 256], P('ch')
- rgate_b: bfloat16 [4096], P('ch')
- igate_w: bfloat16 [16, 256, 256], P('ch')
- igate_b: bfloat16 [4096], P('ch')
- w_o: bfloat16 [4096, 4096], P('ch', 'wd')
- bias_o: bfloat16 [4096], P('wd')
- gain_mlp: bfloat16 [4096], P('wd')
- w_g: bfloat16 [4096, 12288], P('wd', 'ch')
- bias_g: bfloat16 [12288], P('ch')
- w_u: bfloat16 [4096, 12288], P('wd', 'ch')
- bias_u: bfloat16 [12288], P('ch')
- w_d: bfloat16 [12288, 4096], P('ch', 'wd')
- bias_d: bfloat16 [4096], P('wd')
Outputs:
- output: bfloat16 [8192, 4096], P('dp', 'wd'), parts along dimension 0
There are 2 independent parts. A program takes and returns all parts, laid end to end along the dimension named above; an argument that names none is the same for every part.
All inputs are finite; a program needn't handle non-finite values.
Results may differ from a plain program's by a relative error of at most 0.0129929.
Values are sent between devices in bfloat16 or wider.
A program may use at most 1 GiB of HBM per device.

v0:
```python
import jax
import jax.numpy as jnp
from jax import lax
from jax.sharding import PartitionSpec as P, NamedSharding

EPS = 1e-6


def rms_apply(vals, sum_sq, width, gain):
    return (vals * lax.rsqrt(sum_sq / width + EPS) * (1.0 + gain.astype(jnp.float32))).astype(jnp.bfloat16)


def token_sum(part_sum, axis_name, count):
    tokens, width = part_sum.shape
    pieces = part_sum.astype(jnp.bfloat16).reshape(count, tokens // count, width)
    received = lax.all_to_all(pieces, axis_name, 0, 0)
    return jnp.sum(received.astype(jnp.float32), axis=0)


def conv_mix(vals, positions, conv_w, conv_bias):
    vals32 = vals.astype(jnp.float32)
    taps = conv_w.astype(jnp.float32)
    total = conv_bias.astype(jnp.float32) + vals32 * taps[0]
    for shift in range(1, conv_w.shape[0]):
        moved = jnp.pad(vals32[:-shift], ((shift, 0), (0, 0)))
        total = total + jnp.where((positions >= shift)[:, None], moved, 0.0) * taps[shift]
    return total.astype(jnp.bfloat16)


def combine(left, right):
    return left[0] * right[0], right[0] * left[1] + right[1]


def rg_lru(conv_out, positions, seqs, lam_param, rgate_w, rgate_b, igate_w, igate_b):
    tokens, width = conv_out.shape
    blocks = rgate_w.shape[0]
    grouped = conv_out.reshape(tokens, blocks, width // blocks)
    rate = jax.nn.sigmoid(jnp.einsum('nbi,bij->nbj', grouped, rgate_w, preferred_element_type=jnp.float32).reshape(tokens, width) + rgate_b.astype(jnp.float32))
    inflow = jax.nn.sigmoid(jnp.einsum('nbi,bij->nbj', grouped, igate_w, preferred_element_type=jnp.float32).reshape(tokens, width) + igate_b.astype(jnp.float32))
    log_a = -8.0 * rate * jax.nn.softplus(-lam_param)
    reset = (positions == 0)[:, None]
    decay = jnp.where(reset, 0.0, jnp.exp(log_a))
    scale = jnp.where(reset, 1.0, jnp.sqrt(-jnp.expm1(2.0 * log_a)))
    drive = scale * inflow * conv_out.astype(jnp.float32)
    steps = tokens // seqs
    hidden = lax.associative_scan(combine, (decay.reshape(seqs, steps, width), drive.reshape(seqs, steps, width)), axis=1)[1]
    return hidden.reshape(tokens, width)


def solution(mesh):
    wd_count = mesh.shape['wd']
    ch_count = mesh.shape['ch']
    row_spec = P('dp', 'wd')
    specs = (row_spec, P('dp', None), P('wd'), P('wd', 'ch'), P('ch'), P('wd', 'ch'), P('ch'), P(None, 'ch'), P('ch'), P('ch'), P('ch', None, None), P('ch'), P('ch', None, None), P('ch'), P('ch', 'wd'), P('wd'), P('wd'), P('wd', 'ch'), P('ch'), P('wd', 'ch'), P('ch'), P('ch', 'wd'), P('wd'))

    def local_layer(resid_in, seg_pos, gain_temporal, w_x, bias_x, w_y, bias_y, conv_w, conv_bias, lam_param, rgate_w, rgate_b, igate_w, igate_b, w_o, bias_o, gain_mlp, w_g, bias_g, w_u, bias_u, w_d, bias_d):
        tokens, local_width = resid_in.shape
        model_width = local_width * wd_count
        share = tokens // ch_count
        positions = seg_pos.reshape(tokens)
        resid32 = resid_in.astype(jnp.float32)
        sum_sq = lax.psum(jnp.sum(resid32 * resid32, axis=1, keepdims=True), 'wd')
        normed = rms_apply(resid32, sum_sq, model_width, gain_temporal)
        y_sum = token_sum(jnp.dot(normed, w_y, preferred_element_type=jnp.float32), 'wd', wd_count)
        y_rows = jax.nn.gelu(y_sum + bias_y.astype(jnp.float32), approximate=True).astype(jnp.bfloat16)
        y_branch = lax.all_gather(y_rows, 'wd', axis=0, tiled=True)
        u_sum = token_sum(jnp.dot(normed, w_x, preferred_element_type=jnp.float32), 'wd', wd_count)
        u_rows = (u_sum + bias_x.astype(jnp.float32)).astype(jnp.bfloat16)
        u_branch = lax.all_gather(u_rows, 'wd', axis=0, tiled=True)
        conv_out = conv_mix(u_branch, positions, conv_w, conv_bias)
        hidden = rg_lru(conv_out, positions, seg_pos.shape[0], lam_param, rgate_w, rgate_b, igate_w, igate_b)
        mixed = (hidden * y_branch.astype(jnp.float32)).astype(jnp.bfloat16)
        mix_sum = token_sum(jnp.dot(mixed, w_o, preferred_element_type=jnp.float32), 'ch', ch_count)
        resid_rows = lax.dynamic_slice_in_dim(resid32, lax.axis_index('ch') * share, share, axis=0)
        resid = resid_rows + mix_sum + bias_o.astype(jnp.float32)
        sum_sq2 = lax.psum(jnp.sum(resid * resid, axis=1, keepdims=True), 'wd')
        normed2 = lax.all_gather(rms_apply(resid, sum_sq2, model_width, gain_mlp), 'ch', axis=0, tiled=True)
        gate_sum = token_sum(jnp.dot(normed2, w_g, preferred_element_type=jnp.float32), 'wd', wd_count)
        up_sum = token_sum(jnp.dot(normed2, w_u, preferred_element_type=jnp.float32), 'wd', wd_count)
        inner_rows = (jax.nn.gelu(gate_sum + bias_g.astype(jnp.float32), approximate=True) * (up_sum + bias_u.astype(jnp.float32))).astype(jnp.bfloat16)
        inner = lax.all_gather(inner_rows, 'wd', axis=0, tiled=True)
        down_sum = token_sum(jnp.dot(inner, w_d, preferred_element_type=jnp.float32), 'ch', ch_count)
        out_rows = (resid + down_sum + bias_d.astype(jnp.float32)).astype(jnp.bfloat16)
        return lax.all_gather(out_rows, 'ch', axis=0, tiled=True)

    return jax.shard_map(local_layer, mesh=mesh, in_specs=specs, out_specs=row_spec, check_vma=False)
```

profile of v0, /device:TPU:0, one launch (start us, length us, event | category | flops | bytes accessed | tf_op | source)
XLA Modules:
  0.0 2856.4 jit_solution(11413349695447939007)
XLA Ops:
  12.5 12.7 psum.14
  25.2 14.7 convolution_convert_fusion.3
  46.3 92.2 %all-to-all-done = bf16[4,1024,1024]{2,1,0:T(8,128)(2,1)} async-done(((bf16[4,1024,1024]{2,1,0:T(8,128)(2,1)}), bf16[4,1024,1024]{2,1,0:T(8,128)(2,1)}, u32[]{:S(2)}, u32[]{:S(2)}) %all-to-all-start) | async-done | bytes 8388640 | tf_op jit(solution)/shard_map/all_to_all | solution.py:16
  146.5 15.0 convolution_convert_fusion.2
  167.9 125.7 %all-to-all-done.1 = bf16[4,1024,1024]{2,1,0:T(8,128)(2,1)} async-done(((bf16[4,1024,1024]{2,1,0:T(8,128)(2,1)}), bf16[4,1024,1024]{2,1,0:T(8,128)(2,1)}, u32[]{:S(2)}, u32[]{:S(2)}) %all-to-all-start.1) | async-done | bytes 8388640 | tf_op jit(solution)/shard_map/all_to_all | solution.py:16
  336.2 24.6 add_convert_fusion
  372.0 11.5 fusion.51
  383.5 17.5 copy.36
  401.0 11.5 fusion.50
  412.6 17.5 copy.33
  430.0 17.5 copy.37
  447.5 28.2 multiply_bitcast_fusion
  485.6 36.6 %slice.308 = f32[1,2047,1024]{2,1,0:T(8,128)} slice(f32[1,4096,1024]{2,1,0:T(8,128)} %exponential_select_fusion), slice={[0:1:1], [2:4096:2], [0:1024:1]} | slice | bytes 16769024 | tf_op jit(solution)/shard_map/slice | solution.py:46
  522.2 36.0 %slice.313 = f32[1,2048,1024]{2,1,0:T(8,128)} slice(f32[1,4096,1024]{2,1,0:T(8,128)} %exponential_select_fusion), slice={[0:1:1], [0:4095:2], [0:1024:1]} | slice | bytes 16777216 | tf_op jit(solution)/shard_map/slice | solution.py:46
  558.2 36.0 %slice.309 = f32[1,2048,1024]{2,1,0:T(8,128)} slice(f32[1,4096,1024]{2,1,0:T(8,128)} %exponential_select_fusion), slice={[0:1:1], [1:4096:2], [0:1024:1]} | slice | bytes 16777216 | tf_op jit(solution)/shard_map/slice | solution.py:46
  594.2 36.6 %slice.397 = f32[1,2047,1024]{2,1,0:T(8,128)} slice(f32[1,4096,1024]{2,1,0:T(8,128)} %multiply_bitcast_fusion), slice={[0:1:1], [2:4096:2], [0:1024:1]} | slice | bytes 16769024 | tf_op jit(solution)/shard_map/slice | solution.py:46
  630.8 36.1 %slice.311 = f32[1,2048,1024]{2,1,0:T(8,128)} slice(f32[1,4096,1024]{2,1,0:T(8,128)} %multiply_bitcast_fusion), slice={[0:1:1], [1:4096:2], [0:1024:1]} | slice | bytes 16777216 | tf_op jit(solution)/shard_map/slice | solution.py:46
  666.9 36.0 %slice.310 = f32[1,2048,1024]{2,1,0:T(8,128)} slice(f32[1,4096,1024]{2,1,0:T(8,128)} %multiply_bitcast_fusion), slice={[0:1:1], [0:4095:2], [0:1024:1]} | slice | bytes 16777216 | tf_op jit(solution)/shard_map/slice | solution.py:46
  702.9 18.7 fusion.37
  721.6 18.5 slice.319
  740.1 18.5 slice.315
  758.6 18.5 slice.317
  777.1 18.5 slice.316
  795.7 12.2 fusion.38
  976.1 19.0 slice.395
  995.1 19.0 slice.314
  1043.3 16.6 pad.106
  1075.7 32.4 %pad.109 = f32[1,2048,1024]{2,1,0:T(8,128)} pad(f32[1,1024,1024]{2,1,0:T(8,128)} %add.370, f32[]{:T(128)} %constant.23.clone.1), padding=0_0_0x1_0_1x0_0_0 | pad | bytes 12582916 | tf_op jit(solution)/shard_map/pad | solution.py:46
  1118.6 32.5 %pad.108 = f32[1,2048,1024]{2,1,0:T(8,128)} pad(f32[1,1024,1024]{2,1,0:T(8,128)} %pad_maximum_fusion.1, f32[]{:T(128)} %constant.23.clone.1), padding=0_0_0x0_1_1x0_0_0 | pad | bytes 12582916 | tf_op jit(solution)/shard_map/pad | solution.py:46
  1151.0 12.0 add.372
  1163.0 12.7 fusion.12
  1180.2 64.0 %pad.110 = f32[1,4096,1024]{2,1,0:T(8,128)} pad(f32[1,2048,1024]{2,1,0:T(8,128)} %pad_maximum_fusion, f32[]{:T(128)} %constant.23.clone.1), padding=0_0_0x0_1_1x0_0_0 | pad | bytes 25165828 | tf_op jit(solution)/shard_map/pad | solution.py:46
  1244.2 64.2 %pad.111 = f32[1,4096,1024]{2,1,0:T(8,128)} pad(f32[1,2048,1024]{2,1,0:T(8,128)} %add.372, f32[]{:T(128)} %constant.23.clone.1), padding=0_0_0x1_0_1x0_0_0 | pad | bytes 25165828 | tf_op jit(solution)/shard_map/pad | solution.py:46
  1308.4 20.2 fusion.13
  1334.3 11.3 convert_element_type.114
  1345.6 171.7 %all-to-all-done.2 = bf16[4,1024,1024]{2,1,0:T(8,128)(2,1)} async-done(((bf16[4,1024,1024]{2,1,0:T(8,128)(2,1)}), bf16[4,1024,1024]{2,1,0:T(8,128)(2,1)}, u32[]{:S(2)}, u32[]{:S(2)}) %all-to-all-start.2) | async-done | bytes 8388640 | tf_op jit(solution)/shard_map/all_to_all | solution.py:16
  1538.0 148.0 %all-gather.10.cloned.1.call-done = bf16[4096,1024]{1,0:T(8,128)(2,1)} async-done(((bf16[1024,1024]{1,0:T(8,128)(2,1)}), bf16[4096,1024]{1,0:T(8,128)(2,1)}) %all-gather.10.cloned.1.call-update) | async-done | bytes 8388624 | tf_op jit(solution)/shard_map/all_gather | solution.py:77
  1686.0 34.2 %convolution_convert_fusion = bf16[4096,3072]{1,0:T(8,128)(2,1)} fusion(bf16[4096,1024]{1,0:T(8,128)(2,1)} %all-gather.10.cloned.1.call-done, bf16[1024,3072]{1,0:T(8,128)(2,1)} %param.42), kind=kOutput, calls=%fused_computation.2 | convolution fusion | flops 25782386688 | bytes 39845888 | tf_op jit(solution)/shard_map/dot_general | solution.py:79
  1728.8 34.2 %convolution_convert_fusion.1 = bf16[4096,3072]{1,0:T(8,128)(2,1)} fusion(bf16[4096,1024]{1,0:T(8,128)(2,1)} %all-gather.10.cloned.1.call-done, bf16[1024,3072]{1,0:T(8,128)(2,1)} %param.40), kind=kOutput, calls=%fused_computation.3 | convolution fusion | flops 25782386688 | bytes 39845888 | tf_op jit(solution)/shard_map/dot_general | solution.py:78
  1763.0 238.4 %all-to-all-done.4 = bf16[4,1024,3072]{2,1,0:T(8,128)(2,1)} async-done(((bf16[4,1024,3072]{2,1,0:T(8,128)(2,1)}), bf16[4,1024,3072]{2,1,0:T(8,128)(2,1)}, u32[]{:S(2)}, u32[]{:S(2)}) %all-to-all-start.4) | async-done | bytes 25165856 | tf_op jit(solution)/shard_map/all_to_all | solution.py:16
  2010.2 14.3 convert_reduce_fusion
  2024.6 257.9 %all-to-all-done.3 = bf16[4,1024,3072]{2,1,0:T(8,128)(2,1)} async-done(((bf16[4,1024,3072]{2,1,0:T(8,128)(2,1)}), bf16[4,1024,3072]{2,1,0:T(8,128)(2,1)}, u32[]{:S(2)}, u32[]{:S(2)}) %all-to-all-start.3) | async-done | bytes 25165856 | tf_op jit(solution)/shard_map/all_to_all | solution.py:16
  2282.5 14.3 convert_reduce_fusion.1
  2296.8 13.3 fusion.9
  2310.1 153.3 %all-gather.12.cloned.1.call-done = bf16[4096,3072]{1,0:T(8,128)(2,1)} async-done(((bf16[1024,3072]{1,0:T(8,128)(2,1)}), bf16[4096,3072]{1,0:T(8,128)(2,1)}) %all-gather.12.cloned.1.call-update) | async-done | bytes 25165840 | tf_op jit(solution)/shard_map/all_gather | solution.py:81
  2463.4 32.5 %convolution_convert_fusion.4 = bf16[4096,1024]{1,0:T(8,128)(2,1)} fusion(bf16[4096,3072]{1,0:T(8,128)(2,1)} %all-gather.12.cloned.1.call-done, bf16[3072,1024]{1,0:T(8,128)(2,1)} %param.44), kind=kOutput, calls=%fused_computation.33 | convolution fusion | flops 25773998080 | bytes 39845888 | tf_op jit(solution)/shard_map/dot_general | solution.py:82
  2502.1 183.0 %all-to-all-done.5 = bf16[4,1024,1024]{2,1,0:T(8,128)(2,1)} async-done(((bf16[4,1024,1024]{2,1,0:T(8,128)(2,1)}), bf16[4,1024,1024]{2,1,0:T(8,128)(2,1)}, u32[]{:S(2)}, u32[]{:S(2)}) %all-to-all-start.5) | async-done | bytes 8388640 | tf_op jit(solution)/shard_map/all_to_all | solution.py:16
  2693.7 147.9 %all-gather.14.cloned.1.call-done = bf16[4096,1024]{1,0:T(8,128)(2,1)} async-done(((bf16[1024,1024]{1,0:T(8,128)(2,1)}), bf16[4096,1024]{1,0:T(8,128)(2,1)}) %all-gather.14.cloned.1.call-update) | async-done | bytes 8388624 | tf_op jit(solution)/shard_map/all_gather | solution.py:84
  (251 shorter events, 384.0 us)
Async XLA Ops:
  6.5 18.7 copy-start
  39.9 6.4 copy-start.31
  39.9 98.6 %all-to-all-start = ((bf16[4,1024,1024]{2,1,0:T(8,128)(2,1)}), bf16[4,1024,1024]{2,1,0:T(8,128)(2,1)}, u32[]{:S(2)}, u32[]{:S(2)}) async-start(bf16[4,1024,1024]{2,1,0:T(8,128)(2,1)} %bitcast.55), calls=%async_computation | async-start | bytes 16777216 | tf_op jit(solution)/shard_map/all_to_all | solution.py:16
  45.7 256.6 %all-gather.6.cloned.1.call-start = ((), (), s32[]{:S(2)}) async-start(), calls=%async_computation.6 | async-start | bytes 10485760 | tf_op jit(solution)/shard_map/all_gather | solution.py:69
  161.5 6.1 copy-start.33
  161.5 6.1 copy-start.34
  161.5 6.1 copy-start.35
  161.5 6.2 copy-start.27
  161.5 6.3 copy-start.30
  161.5 6.4 copy-start.20
  161.6 132.1 %all-to-all-start.1 = ((bf16[4,1024,1024]{2,1,0:T(8,128)(2,1)}), bf16[4,1024,1024]{2,1,0:T(8,128)(2,1)}, u32[]{:S(2)}, u32[]{:S(2)}) async-start(bf16[4,1024,1024]{2,1,0:T(8,128)(2,1)} %bitcast.53), calls=%async_computation.1 | async-start | bytes 16777216 | tf_op jit(solution)/shard_map/all_to_all | solution.py:16
  167.4 1141.0 %all-gather.8.cloned.1.call-start = ((), (), s32[]{:S(2)}) async-start(), calls=%async_computation.7 | async-start | bytes 10485760 | tf_op jit(solution)/shard_map/all_gather | solution.py:66
  360.8 11.2 copy-start.8
  383.5 17.5 copy-start.9
  447.5 28.2 copy-start.2
  976.0 39.6 %copy-start.19 = (f32[1,2,1024]{2,1,0:T(2,128)S(1)}, f32[1,2,1024]{2,1,0:T(2,128)}, u32[]{:S(2)}) copy-start(f32[1,2,1024]{2,1,0:T(2,128)} %slice.369) | copy-start | bytes 24580
  976.0 39.6 %copy-start.21 = (f32[1,2,1024]{2,1,0:T(2,128)S(1)}, f32[1,2,1024]{2,1,0:T(2,128)}, u32[]{:S(2)}) copy-start(f32[1,2,1024]{2,1,0:T(2,128)} %slice.371) | copy-start | bytes 24580
  976.0 39.6 %copy-start.22 = (f32[1,2,1024]{2,1,0:T(2,128)S(1)}, f32[1,2,1024]{2,1,0:T(2,128)}, u32[]{:S(2)}) copy-start(f32[1,2,1024]{2,1,0:T(2,128)} %slice.370) | copy-start | bytes 24580
  976.0 39.6 %copy-start.23 = (f32[1,2,1024]{2,1,0:T(2,128)S(1)}, f32[1,2,1024]{2,1,0:T(2,128)}, u32[]{:S(2)}) copy-start(f32[1,2,1024]{2,1,0:T(2,128)} %slice.373) | copy-start | bytes 24580
  976.0 40.5 %copy-start.17 = (f32[1,3,1024]{2,1,0:T(4,128)S(1)}, f32[1,3,1024]{2,1,0:T(4,128)}, u32[]{:S(2)}) copy-start(f32[1,3,1024]{2,1,0:T(4,128)} %slice.379) | copy-start | bytes 36868
  976.0 40.5 %copy-start.18 = (f32[1,3,1024]{2,1,0:T(4,128)S(1)}, f32[1,3,1024]{2,1,0:T(4,128)}, u32[]{:S(2)}) copy-start(f32[1,3,1024]{2,1,0:T(4,128)} %slice.362) | copy-start | bytes 36868
  976.1 40.5 %copy-start.26 = (f32[1,1,1024]{2,1,0:T(1,128)S(1)}, f32[1,1,1024]{2,1,0:T(1,128)}, u32[]{:S(2)}) copy-start(f32[1,1,1024]{2,1,0:T(1,128)} %slice.414) | copy-start | bytes 12292
  976.1 40.6 %copy-start.15 = (f32[1,7,1024]{2,1,0:T(8,128)S(1)}, f32[1,7,1024]{2,1,0:T(8,128)}, u32[]{:S(2)}) copy-start(f32[1,7,1024]{2,1,0:T(8,128)} %slice.356) | copy-start | bytes 86020
  976.1 40.6 %copy-start.16 = (f32[1,7,1024]{2,1,0:T(8,128)S(1)}, f32[1,7,1024]{2,1,0:T(8,128)}, u32[]{:S(2)}) copy-start(f32[1,7,1024]{2,1,0:T(8,128)} %slice.381) | copy-start | bytes 86020
  976.1 40.6 %copy-start.25 = (f32[1,1,1024]{2,1,0:T(1,128)S(1)}, f32[1,1,1024]{2,1,0:T(1,128)}, u32[]{:S(2)}) copy-start(f32[1,1,1024]{2,1,0:T(1,128)} %slice.413) | copy-start | bytes 12292
  976.1 40.7 %copy-start.13 = (f32[1,15,1024]{2,1,0:T(8,128)S(1)}, f32[1,15,1024]{2,1,0:T(8,128)}, u32[]{:S(2)}) copy-start(f32[1,15,1024]{2,1,0:T(8,128)} %slice.383) | copy-start | bytes 184324
  976.1 40.7 %copy-start.14 = (f32[1,15,1024]{2,1,0:T(8,128)S(1)}, f32[1,15,1024]{2,1,0:T(8,128)}, u32[]{:S(2)}) copy-start(f32[1,15,1024]{2,1,0:T(8,128)} %slice.350) | copy-start | bytes 184324
  976.1 40.7 %copy-start.24 = (f32[1,1,1024]{2,1,0:T(1,128)S(1)}, f32[1,1,1024]{2,1,0:T(1,128)}, u32[]{:S(2)}) copy-start(f32[1,1,1024]{2,1,0:T(1,128)} %slice.412) | copy-start | bytes 12292
  976.1 40.8 %copy-start.11 = (f32[1,31,1024]{2,1,0:T(8,128)S(1)}, f32[1,31,1024]{2,1,0:T(8,128)}, u32[]{:S(2)}) copy-start(f32[1,31,1024]{2,1,0:T(8,128)} %slice.344) | copy-start | bytes 380932
  976.1 40.8 %copy-start.12 = (f32[1,31,1024]{2,1,0:T(8,128)S(1)}, f32[1,31,1024]{2,1,0:T(8,128)}, u32[]{:S(2)}) copy-start(f32[1,31,1024]{2,1,0:T(8,128)} %slice.385) | copy-start | bytes 380932
  995.1 22.1 copy-start.10
  995.1 23.2 copy-start.6
  995.1 23.2 copy-start.7
  1041.7 18.3 copy-start.5
  1244.2 64.2 %copy-start.39 = (bf16[1024,1024]{1,0:T(8,128)(2,1)S(1)}, bf16[1024,1024]{1,0:T(8,128)(2,1)}, u32[]{:S(2)}) copy-start(bf16[1024,1024]{1,0:T(8,128)(2,1)} %param.37) | copy-start | bytes 6291460
  1328.5 188.8 %all-to-all-start.2 = ((bf16[4,1024,1024]{2,1,0:T(8,128)(2,1)}), bf16[4,1024,1024]{2,1,0:T(8,128)(2,1)}, u32[]{:S(2)}, u32[]{:S(2)}) async-start(bf16[4,1024,1024]{2,1,0:T(8,128)(2,1)} %bitcast.52), calls=%async_computation.2 | async-start | bytes 16777216 | tf_op jit(solution)/shard_map/all_to_all | solution.py:16
  1334.2 11.4 copy-start.36
  1334.2 11.4 copy-start.37
  1334.2 351.8 %all-gather.10.cloned.1.call-start = ((), (), s32[]{:S(2)}) async-start(), calls=%async_computation.8 | async-start | bytes 10485760 | tf_op jit(solution)/shard_map/all_gather | solution.py:77
  1720.2 281.2 %all-to-all-start.4 = ((bf16[4,1024,3072]{2,1,0:T(8,128)(2,1)}), bf16[4,1024,3072]{2,1,0:T(8,128)(2,1)}, u32[]{:S(2)}, u32[]{:S(2)}) async-start(bf16[4,1024,3072]{2,1,0:T(8,128)(2,1)} %bitcast.51), calls=%async_computation.4 | async-start | bytes 50331648 | tf_op jit(solution)/shard_map/all_to_all | solution.py:16
  2001.4 8.8 copy-start.28
  2001.4 8.8 copy-start.29
  2001.4 281.1 %all-to-all-start.3 = ((bf16[4,1024,3072]{2,1,0:T(8,128)(2,1)}), bf16[4,1024,3072]{2,1,0:T(8,128)(2,1)}, u32[]{:S(2)}, u32[]{:S(2)}) async-start(bf16[4,1024,3072]{2,1,0:T(8,128)(2,1)} %bitcast.50), calls=%async_computation.3 | async-start | bytes 50331648 | tf_op jit(solution)/shard_map/all_to_all | solution.py:16
  2009.9 453.5 %all-gather.12.cloned.1.call-start = ((), (), s32[]{:S(2)}) async-start(), calls=%async_computation.9 | async-start | bytes 31457280 | tf_op jit(solution)/shard_map/all_gather | solution.py:81
  2496.0 6.1 copy-start.38
  2496.0 189.2 %all-to-all-start.5 = ((bf16[4,1024,1024]{2,1,0:T(8,128)(2,1)}), bf16[4,1024,1024]{2,1,0:T(8,128)(2,1)}, u32[]{:S(2)}, u32[]{:S(2)}) async-start(bf16[4,1024,1024]{2,1,0:T(8,128)(2,1)} %bitcast.54), calls=%async_computation.5 | async-start | bytes 16777216 | tf_op jit(solution)/shard_map/all_to_all | solution.py:16
  2501.8 339.9 %all-gather.14.cloned.1.call-start = ((), (), s32[]{:S(2)}) async-start(), calls=%async_computation.10 | async-start | bytes 10485760 | tf_op jit(solution)/shard_map/all_gather | solution.py:84
  2693.7 155.7 %copy-start.1 = (bf16[1024,1024]{1,0:T(8,128)(2,1)S(1)}, bf16[1024,1024]{1,0:T(8,128)(2,1)}, u32[]{:S(2)}) copy-start(bf16[1024,1024]{1,0:T(8,128)(2,1)} %param.26) | copy-start | bytes 6291460
  (3 other events, 13.2 us)
Sparse Core Ops, SparseCore 0:
  146.6 92.5 all-gather.5
  302.4 58.4 all-gather.7
  1538.1 147.8 all-gather.9
  2310.3 153.1 all-gather.11
  2693.8 147.7 all-gather.13
where the time goes:
time: 2880 us; the launch traced here: 2860 us
  waiting for transfers between devices  1520 us (53%)
  local copies, waits for them, and re-layouts  815 us (28%)
  other arithmetic  274 us (10%)
  matrix products  174 us (6%)
  starting transfers between devices  41.6 us (1%)
    all_to_all x6, waiting for transfers between devices, token_sum(): received = lax.all_to_all(pieces, axis_name, 0, 0)  1070 us
    slice x74, local copies, waits for them, and re-layouts, rg_lru(): lax.associative_scan(combine, (decay.reshape(seqs, steps, width), drive.r...  478 us
    pad x22, local copies, waits for them, and re-layouts, rg_lru(): lax.associative_scan(combine, (decay.reshape(seqs, steps, width), drive.r...  230 us
    all_gather x1, waiting for transfers between devices, local_layer(): inner = lax.all_gather(inner_rows, 'wd', axis=0, tiled=True)  153 us
    all_gather x1, waiting for transfers between devices, local_layer(): lax.all_gather(rms_apply(resid, sum_sq2, model_width, gain_mlp), 'ch', ax...  148 us
    all_gather x1, waiting for transfers between devices, local_layer(): return lax.all_gather(out_rows, 'ch', axis=0, tiled=True)  148 us
  transfers between devices with their start and end apart: 11, of which 9 were waited for; matrix products, arithmetic and copies ran while one was open for 38% of the time, Pallas kernels for 0%

commit v1 on v0

v1 whole, which is shorter than its diff:
```python
import functools

import jax
import jax.numpy as jnp
from jax import lax
from jax.experimental import pallas as pl
from jax.experimental.pallas import tpu as pltpu
from jax.sharding import PartitionSpec as P


EPS = 1e-6
CHUNKS = 2
SUB = 16
TILE = 256
PIECES = 4
GROUP = 8
WAYS = (0, 1)
BLOCKS = (0, 1, 2, 3)
OTHERS = BLOCKS[1:]
LIMIT = 60 * 2 ** 20
WORK = pl.CostEstimate(flops=2 * 10 ** 11, bytes_accessed=2 * 10 ** 7, transcendentals=0)
MESH = pl.DeviceIdType.MESH
F32 = jnp.float32
BF16 = jnp.bfloat16


def flip_pairs(count, r):
    return [(i, i ^ r) for i in range(count)]


def dot32(a, b):
    return jnp.dot(a, b, preferred_element_type=F32)


def lru_body(idx_ref, own_ref, peer_ref, far_ref, pos_ref, bias_ref, conv_ref, sp_ref, gate_w_ref, gate_b_ref, tail_ref, carry_ref, mixed_ref, tail_out, carry_out, ubuf, abuf, bbuf, carry):
    step = pl.program_id(0)
    rows, width = abuf.shape

    @pl.when(step == 0)
    def _():
        ubuf[:GROUP, :] = tail_ref[...]
        carry[...] = carry_ref[...]

    @pl.when(step > 0)
    def _():
        ubuf[:GROUP, :] = ubuf[rows:, :]

    total = own_ref[...].astype(F32) + peer_ref[...].astype(F32) + far_ref[...].astype(F32) + bias_ref[...]
    ubuf[GROUP:, :] = total[:, :width].astype(BF16).astype(F32)
    pos = pos_ref[...]
    conv = conv_ref[4:5, :] + ubuf[GROUP:, :] * conv_ref[0:1, :]
    for shift in OTHERS:
        moved = ubuf[GROUP - shift:rows + GROUP - shift, :]
        conv = conv + jnp.where(pos >= shift, moved, 0.0) * conv_ref[shift:shift + 1, :]
    conv_b = conv.astype(BF16)
    conv32 = conv_b.astype(F32)
    gates = jax.nn.sigmoid(dot32(conv_b, gate_w_ref[...]) + gate_b_ref[...])
    rate = gates[:, :width]
    inflow = gates[:, width:]
    depth = 8.0 * rate * sp_ref[...]
    twice = 2.0 * depth
    series = 1.0
    for k in (5, 4, 3, 2):
        series = 1.0 - (twice * series) / k
    series = twice * series
    left = jnp.where(twice < 0.125, series, 1.0 - jnp.exp(-twice))
    reset = pos == 0
    abuf[...] = jnp.where(reset, 0.0, jnp.exp(-depth))
    bbuf[...] = jnp.where(reset, 1.0, jnp.sqrt(left)) * inflow * conv32

    row = lax.broadcasted_iota(jnp.int32, (GROUP, width), 0)

    def group(g, held):
        at = pl.multiple_of(g * GROUP, GROUP)
        a = abuf[pl.ds(at, GROUP), :]
        b = bbuf[pl.ds(at, GROUP), :]
        for d in (1, 2, 4):
            keep = row >= d
            b = b + a * jnp.where(keep, pltpu.roll(b, d, 0), 0.0)
            a = a * jnp.where(keep, pltpu.roll(a, d, 0), 1.0)
        bbuf[pl.ds(at, GROUP), :] = b + a * held
        last_a = jnp.broadcast_to(a[GROUP - 1:, :], (GROUP, width))
        last_b = jnp.broadcast_to(b[GROUP - 1:, :], (GROUP, width))
        return last_b + last_a * held

    held = lax.fori_loop(0, rows // GROUP, group, carry[...], unroll=GROUP)
    carry[...] = held
    y_branch = jax.nn.gelu(total[:, width:], approximate=True).astype(BF16)
    mixed_ref[...] = (bbuf[...] * y_branch.astype(F32)).astype(BF16).reshape(mixed_ref.shape)
    tail_out[...] = ubuf[rows:, :]
    carry_out[...] = held


def lru(idx, own, peer, far, pos, bias, conv, sp, gate_w, gate_b, tail, carry, rows):
    tokens = own.shape[0]
    width = own.shape[1] // 2
    blocks = tokens // rows
    wide = pl.BlockSpec((rows, 2 * width), lambda s, idx: (s, 0))
    full = lambda arr: pl.BlockSpec(arr.shape, lambda s, idx: (0,) * arr.ndim)
    state = jax.ShapeDtypeStruct((GROUP, width), F32)
    return pl.pallas_call(
        lru_body,
        grid_spec=pltpu.PrefetchScalarGridSpec(
            num_scalar_prefetch=1,
            grid=(blocks,),
            in_specs=[wide, wide, wide, pl.BlockSpec((rows, 1), lambda s, idx: (s, 0))] + [full(v) for v in (bias, conv, sp, gate_w, gate_b, tail, carry)],
            out_specs=[pl.BlockSpec((1, 1, rows, width), lambda s, idx: ((s % 4) ^ idx[0], s // 4, 0, 0)), full(tail), full(carry)],
            scratch_shapes=[pltpu.VMEM((rows + GROUP, width), F32), pltpu.VMEM((rows, width), F32), pltpu.VMEM((rows, width), F32), pltpu.VMEM((GROUP, width), F32)],
        ),
        out_shape=[jax.ShapeDtypeStruct((4, blocks // 4, rows, width), BF16), state, state],
        compiler_params=pltpu.CompilerParams(dimension_semantics=("arbitrary",)),
        cost_estimate=pl.CostEstimate(flops=tokens * width * 4000, bytes_accessed=tokens * width * 20, transcendentals=tokens * width * 8),
        name="lru",
    )(idx, own, peer, far, pos, bias, conv, sp, gate_w, gate_b, tail, carry)


def pieces_specs(pieces, cols):
    return [pl.BlockSpec((w.shape[0], cols), lambda j, idx: (0, j)) for w in pieces]


def put_rows(out_ref, r, val):
    zs, steps, _, rows, cols = out_ref.shape
    out_ref[:, :, r] = val.astype(BF16).reshape(zs, steps, rows, cols)


def down_body(idx_ref, inner_ref, own, core, far_a, far_b, both_a, both_b, out_ref):
    dp = idx_ref[1]
    half = inner_ref.shape[2]
    put = functools.partial(put_rows, out_ref)
    for r, w in ((0, own), (1, core)):
        put(r, dot32(inner_ref[0], w[0:half, :]) + dot32(inner_ref[1], w[half:2 * half, :]))
    for r, near, far in ((2, far_a, far_b), (3, both_a, both_b)):
        put(r, dot32(inner_ref[dp], near[...]) + dot32(inner_ref[1 - dp], far[...]))


def partial_rows(body, idx, lhs, pieces, grid_rows, cols):
    zs, steps, rows = grid_rows
    depth, width = pieces[0].shape
    return pl.pallas_call(
        body,
        grid_spec=pltpu.PrefetchScalarGridSpec(
            num_scalar_prefetch=1,
            grid=(width // cols,),
            in_specs=[pl.BlockSpec(lhs.shape, lambda j, idx: (0,) * lhs.ndim)] + pieces_specs(pieces, cols),
            out_specs=pl.BlockSpec((zs, steps, 4, rows, cols), lambda j, idx: (0, 0, 0, 0, j)),
        ),
        out_shape=jax.ShapeDtypeStruct((zs, steps, 4, rows, width), BF16),
        compiler_params=pltpu.CompilerParams(dimension_semantics=("arbitrary",)),
        cost_estimate=pl.CostEstimate(flops=2 * zs * steps * rows * depth * 4 * width, bytes_accessed=depth * 4 * width * 2, transcendentals=0),
    )(idx, lhs, *pieces)


def gate_up_body(idx_ref, m_ref, *refs):
    dp = idx_ref[1]
    g_parts, u_parts, (bias_g, bias_u, inner_ref) = refs[:6], refs[6:12], refs[12:]
    zs, steps, _, rows, depth = m_ref.shape
    lhs = lambda k: m_ref[:, :, k].reshape(zs * steps * rows, depth)

    def product(parts):
        own, core, far_a, far_b, both_a, both_b = parts
        acc = dot32(lhs(0), own[0:depth, :]) + dot32(lhs(1), own[depth:2 * depth, :])
        acc = acc + dot32(lhs(2), core[0:depth, :]) + dot32(lhs(3), core[depth:2 * depth, :])
        acc = acc + dot32(lhs(4 + dp), far_a[...]) + dot32(lhs(5 - dp), far_b[...])
        return acc + dot32(lhs(6 + dp), both_a[...]) + dot32(lhs(7 - dp), both_b[...])

    gate = jax.nn.gelu(product(g_parts) + bias_g[...], approximate=True)
    inner_ref[0] = (gate * (product(u_parts) + bias_u[...])).astype(BF16)


def gate_up(idx, m, g_pieces, u_pieces, bias_g, bias_u, cols):
    zs, steps, ks, rows, depth = m.shape
    steps = steps // 2
    toks = zs * steps * rows
    width = g_pieces[0].shape[1]
    tiles = width // cols
    bias_spec = pl.BlockSpec((1, cols), lambda j, idx: (0, j))
    return pl.pallas_call(
        gate_up_body,
        grid_spec=pltpu.PrefetchScalarGridSpec(
            num_scalar_prefetch=1,
            grid=(tiles,),
            in_specs=[pl.BlockSpec((zs, steps, ks, rows, depth), lambda j, idx: (0,) * 5)] + pieces_specs(g_pieces, cols) + pieces_specs(u_pieces, cols) + [bias_spec, bias_spec],
            out_specs=pl.BlockSpec((1, toks, cols), lambda j, idx: (j // (tiles // 2), 0, j % (tiles // 2))),
        ),
        out_shape=jax.ShapeDtypeStruct((2, toks, width // 2), BF16),
        compiler_params=pltpu.CompilerParams(dimension_semantics=("arbitrary",)),
        cost_estimate=pl.CostEstimate(flops=4 * toks * ks * depth * width, bytes_accessed=4 * ks * depth * width, transcendentals=toks * width),
        name="gate_up",
    )(idx, m, *g_pieces, *u_pieces, bias_g, bias_u)


def line_body(kind, n_ship, *refs):
    if kind == "norm":
        x_rows, (bias, gain, mixed), mix_in, o_parts = refs[:4], refs[4:7], refs[7:11], refs[11:17]
        ship, refs = refs[17:17 + n_ship], refs[17 + n_ship:]
        res_ref, out = refs[:2]
        shipped, refs = refs[2:2 + 5 * n_ship], refs[2 + 5 * n_ship:]
        rbuf, obuf, send, recv, loc, w_send, w_recv, part, mixbuf, wo, a_send, a_recv, pre_sem = refs
    else:
        part_a, res_ref, bias, m_all, bias_g, bias_u = refs[:6]
        g_parts, u_parts, d_parts = refs[6:12], refs[12:18], refs[18:24]
        out, rbuf, obuf, send, recv, loc, a_send, a_recv, part, mbuf, inner, wbuf, pre_sem, tile_sem = refs[24:]
    n = rbuf.shape[1] + 1
    steps = rbuf.shape[2]
    z, me, dp = lax.axis_index('ch'), lax.axis_index('wd'), lax.axis_index('dp')
    lag = 0 if kind == "norm" else 1
    wd_to = lambda r: {'wd': me ^ r}
    peers = [wd_to(r) for r in OTHERS] + ([{'dp': 1 - dp}] if kind == "norm" else [])

    barrier = pltpu.get_barrier_semaphore()
    for peer in peers:
        pl.semaphore_signal(barrier, inc=1, device_id=peer, device_id_type=MESH)

    @pl.when(z > 0)
    def _():
        pl.semaphore_signal(barrier, inc=1, device_id={'ch': z - 1}, device_id_type=MESH)

    @pl.when(z < n - 1)
    def _():
        pl.semaphore_signal(barrier, inc=1, device_id={'ch': z + 1}, device_id_type=MESH)

    @pl.when((z > 0) & (z < n - 1))
    def _():
        pl.semaphore_wait(barrier, len(peers) + 2)

    @pl.when((z == 0) | (z == n - 1))
    def _():
        pl.semaphore_wait(barrier, len(peers) + 1)

    place = lambda way: z if way == 0 else n - 1 - z
    there = lambda way, p: p if way == 0 else n - 1 - p

    def hop(way, slot, s, src, dst):
        return pltpu.make_async_remote_copy(src_ref=src, dst_ref=dst, send_sem=send.at[way, slot, s], recv_sem=recv.at[way, slot, s], device_id={'ch': there(way, jnp.minimum(place(way) + 1, n - 1))}, device_id_type=MESH)

    def reduce_hop(way, h, s, first):
        src = part.at[there(way, place(way) + n - h), s] if first else rbuf.at[way, h - 2, s]
        return hop(way, h - 1, s, src, rbuf.at[way, h - 1, s])

    def reduce_wait(way, h, s):
        at = rbuf.at[way, h - 1, s]
        hop(way, h - 1, s, at, at).wait_recv()

    def block_at(o, s):
        return out.at[o, s] if kind == "norm" else out.at[o, :, s]

    def gather_hop(way, h, s):
        at = block_at(there(way, place(way) - (h - 1)), s)
        src = obuf.at[s] if kind == "norm" and h == 1 else at
        return hop(way, n - 2 + h, s, src, at)

    def local_copy(s):
        src, dst = (obuf.at[s], out.at[z, s]) if kind == "norm" else (obuf.at[s, me], out.at[z, me, s])
        return pltpu.make_async_copy(src, dst, loc.at[s])

    def swap(r, s):
        return pltpu.make_async_remote_copy(src_ref=obuf.at[s, me ^ r], dst_ref=out.at[z, me, s], send_sem=a_send.at[r - 1, s], recv_sem=a_recv.at[r - 1, s], device_id=wd_to(r), device_id_type=MESH)

    def swapped(r, s):
        return pltpu.make_async_remote_copy(src_ref=obuf.at[s, me ^ r], dst_ref=out.at[z, me ^ r, s], send_sem=a_send.at[r - 1, s], recv_sem=a_recv.at[r - 1, s], device_id=wd_to(r), device_id_type=MESH)

    def weight_copy(q, j):
        i, p = q // PIECES, q % PIECES
        far_a, core, both_a, far_b, both_b = shipped[5 * i:5 * i + 5]
        size = far_a.shape[0] // PIECES
        own_at, at = pl.ds((PIECES * dp + p) * size, size), pl.ds(p * size, size)
        if j == 4:
            src, dst = ship[i], core
        elif j == 0:
            src, dst = ship[i].at[own_at], far_a.at[at]
        else:
            src, dst = ((far_a, far_b), (far_a, both_a), (far_b, both_b))[j - 1]
            src, dst = src.at[at], dst.at[at]
        to = (wd_to(2), {'dp': 1 - dp}, wd_to(1), wd_to(1), wd_to(1))[j]
        return pltpu.make_async_remote_copy(src_ref=src, dst_ref=dst, send_sem=w_send.at[q, j], recv_sem=w_recv.at[q, j], device_id=to, device_id_type=MESH)

    def row_places(pieces):
        own, core, far_a, far_b, both_a, both_b = pieces
        size, part_size = own.shape[0], far_a.shape[0]
        return ((own, 0), (core, size), (far_a, 2 * size + dp * part_size), (far_b, 2 * size + (1 - dp) * part_size), (both_a, 3 * size + dp * part_size), (both_b, 3 * size + (1 - dp) * part_size))

    def mix_copy(r, landed):
        there_at = mixbuf.at[me ^ r if landed else me, pl.ds(n - mixed.shape[1], mixed.shape[1])]
        return pltpu.make_async_remote_copy(src_ref=mixed.at[r], dst_ref=there_at, send_sem=a_send.at[r - 1], recv_sem=a_recv.at[r - 1], device_id=wd_to(r), device_id_type=MESH)

    if kind == "norm":
        for r in OTHERS:
            mix_copy(r, False).start()
        jobs = [(mixed.at[0], mixbuf.at[me, pl.ds(n - mixed.shape[1], mixed.shape[1])])]
        jobs += [(src, mixbuf.at[me ^ r, pl.ds(0, src.shape[0])]) for r, src in enumerate(mix_in)]
        jobs += [(w, wo.at[pl.ds(to, w.shape[0])]) for w, to in row_places(o_parts)]
        loads = [pltpu.make_async_copy(src, dst, pre_sem.at[j]) for j, (src, dst) in enumerate(jobs)]
        for copy in loads:
            copy.start()
        for q in range(PIECES * n_ship):
            weight_copy(q, 0).start()
        for i in range(n_ship):
            weight_copy(PIECES * i, 4).start()

        def project(j, _):
            d, r = lax.div(j, 4), lax.rem(j, 4)
            depth = mixbuf.shape[3]
            acc = None
            for b in BLOCKS:
                at = pl.ds(pl.multiple_of((4 * r + b) * depth, depth), depth)
                val = dot32(mixbuf[b, d], wo[at, :])
                acc = val if acc is None else acc + val
            part[d, :, r] = acc.astype(BF16).reshape(steps, part.shape[3], part.shape[4])
            return 0

        for copy in loads:
            copy.wait()
        first = 4 * mix_in[0].shape[0]
        lax.fori_loop(0, first, project, 0)
        for r in OTHERS:
            mix_copy(r, True).wait_recv()
        lax.fori_loop(first, 4 * n, project, 0)

    half = steps // 2
    if kind != "norm":
        gates = inner.shape[1] // TILE
        per_block = part.shape[4] // TILE
        tiles = gates + 4 * per_block
        loads = [pltpu.make_async_copy(part_a, part.at[:, pl.ds(0, half)], pre_sem.at[0]), pltpu.make_async_copy(m_all.at[:, pl.ds(half, half)], mbuf, pre_sem.at[1])]

        def tile_copies(q, down_block):
            slot = lax.rem(q, 2)
            if down_block is None:
                at = pl.ds(pl.multiple_of(q * TILE, TILE), TILE)
                jobs = [(w, i, to) for i, pieces in enumerate((g_parts, u_parts)) for w, to in row_places(pieces)]
            else:
                at = pl.ds(pl.multiple_of(lax.rem(q - gates, per_block) * TILE, TILE), TILE)
                own, core, far_a, far_b, both_a, both_b = d_parts
                rows_a = dp * far_a.shape[0]
                rows_b = far_a.shape[0] - rows_a
                jobs = ([(own, 0, 0)], [(core, 0, 0)], [(far_a, 0, rows_a), (far_b, 0, rows_b)], [(both_a, 0, rows_a), (both_b, 0, rows_b)])[down_block]
            return [pltpu.make_async_copy(w.at[:, at], wbuf.at[slot, i, pl.ds(to, w.shape[0]), :], tile_sem.at[slot, j]) for j, (w, i, to) in enumerate(jobs)]

        def for_tile(q, act):
            @pl.when(q < gates)
            def _():
                for copy in tile_copies(q, None):
                    act(copy)

            for r in BLOCKS:
                @pl.when((q >= gates + r * per_block) & (q < gates + (r + 1) * per_block))
                def _(r=r):
                    for copy in tile_copies(q, r):
                        act(copy)

        def mlp_tile(q, _):
            for_tile(q, lambda copy: copy.wait())
            for_tile(q + 1, lambda copy: copy.start())
            slot = lax.rem(q, 2)
            toks = inner.shape[0]

            @pl.when(q < gates)
            def _():
                at = pl.ds(pl.multiple_of(q * TILE, TILE), TILE)
                sums = []
                for i in range(2):
                    acc = None
                    depth = mbuf.shape[4]
                    for k in range(mbuf.shape[2]):
                        val = dot32(mbuf[:, :, k].reshape(toks, depth), wbuf[slot, i, k * depth:(k + 1) * depth, :])
                        acc = val if acc is None else acc + val
                    sums.append(acc)
                gate = jax.nn.gelu(sums[0] + bias_g[:, at], approximate=True)
                inner[:, at] = (gate * (sums[1] + bias_u[:, at])).astype(BF16)

            @pl.when(q >= gates)
            def _():
                d = q - gates
                at = pl.ds(pl.multiple_of(lax.rem(d, per_block) * TILE, TILE), TILE)
                val = dot32(inner[...], wbuf[slot, 0, 0:inner.shape[1], :]).astype(BF16)
                part[:, pl.ds(half, half), lax.div(d, per_block), :, at] = val.reshape(n, half, part.shape[3], TILE)

            return 0

        for copy in loads:
            copy.start()
        for_tile(0 * z, lambda copy: copy.start())
        for copy in loads:
            copy.wait()

    def finish(s):
        for way in WAYS:
            p = place(way)

            @pl.when(p > 0)
            def _(way=way):
                reduce_wait(way, n - 1, s)

        total = 0.0
        for r in BLOCKS:
            val = part[z, s, r].astype(F32)
            val = val + jnp.where(z > 0, rbuf[0, n - 2, s, r].astype(F32), 0.0)
            val = val + jnp.where(z < n - 1, rbuf[1, n - 2, s, r].astype(F32), 0.0)
            if kind == "norm":
                val = x_rows[r][s].astype(F32) + val + bias[r]
                res_ref[s, r] = val
                total = total + jnp.sum(val * val, axis=1, keepdims=True)
            else:
                obuf[s, me ^ r] = (res_ref[s, r] + val + bias[r]).astype(BF16)
        if kind == "norm":
            width = res_ref.shape[3]
            scale = lax.rsqrt(total / (4 * width) + EPS)
            for r in BLOCKS:
                normed = (res_ref[s, r] * scale * (1.0 + gain[r])).astype(BF16)
                obuf[s, 2 * r] = normed[:, :width // 2]
                obuf[s, 2 * r + 1] = normed[:, width // 2:]
        else:
            for r in OTHERS:
                swap(r, s).start()
        local_copy(s).start()

    def step(t, _):
        for h in range(n, 0, -1):
            s = t - (n - 1) - lag - (h - 1)

            @pl.when((s >= 0) & (s < steps))
            def _(h=h, s=s):
                if h == 1 and kind != "norm":
                    for r in OTHERS:
                        swapped(r, s).wait_recv()
                    local_copy(s).wait()
                if h == 1 and kind == "norm":
                    finish(s)
                for way in WAYS:
                    p = place(way)
                    if h > 1:
                        @pl.when(p >= h - 1)
                        def _(way=way):
                            at = block_at(there(way, place(way) - (h - 1)), s)
                            hop(way, n - 3 + h, s, at, at).wait_recv()
                    if h < n:
                        @pl.when((p >= h - 1) & (p < n - 1))
                        def _(way=way):
                            gather_hop(way, h, s).start()

        if lag:
            s = t - (n - 1)

            @pl.when((s >= 0) & (s < steps))
            def _(s=s):
                finish(s)

        for h in range(n - 1, 0, -1):
            s = t - (h - 1)
            for way in WAYS:
                p = place(way)

                @pl.when((s >= 0) & (s < steps) & (p < h))
                def _(h=h, s=s, way=way, p=p):
                    if h > 1:
                        @pl.when(p > 0)
                        def _():
                            reduce_wait(way, h - 1, s)
                            mine = part[there(way, p + n - h), s].astype(F32)
                            rbuf[way, h - 2, s] = (rbuf[way, h - 2, s].astype(F32) + mine).astype(BF16)
                            reduce_hop(way, h, s, False).start()

                    @pl.when(p == 0)
                    def _():
                        reduce_hop(way, h, s, True).start()

        if kind != "norm":
            @pl.when(t < half)
            def _():
                lax.fori_loop(lax.div(t * tiles, half), lax.div((t + 1) * tiles, half), mlp_tile, 0)

        if kind == "norm":
            for q in range(PIECES * n_ship):
                @pl.when(t == (3 * q + 9) // 2)
                def _(q=q):
                    weight_copy(q, 0).wait_recv()
                    weight_copy(q, 1).start()
                    weight_copy(q, 2).start()

                @pl.when(t == (3 * q + 14) // 2)
                def _(q=q):
                    weight_copy(q, 1).wait_recv()
                    weight_copy(q, 3).start()
        return 0

    lax.fori_loop(0, steps + 2 * n, step, 0)

    def drain(s, _):
        for way in WAYS:
            p = place(way)
            for h in range(1, n):
                @pl.when(p < h)
                def _(way=way, h=h):
                    reduce_hop(way, h, s, True).wait_send()

                @pl.when((p >= h - 1) & (p < n - 1))
                def _(way=way, h=h):
                    gather_hop(way, h, s).wait_send()
        if kind == "norm":
            local_copy(s).wait()
        else:
            for r in OTHERS:
                swap(r, s).wait_send()
        return 0

    lax.fori_loop(0, steps, drain, 0)
    if kind == "norm":
        for q in range(PIECES * n_ship):
            weight_copy(q, 0).wait_send()
            weight_copy(q, 2).wait()
            weight_copy(q, 1).wait_send()
            weight_copy(q, 3).wait()
        for i in range(n_ship):
            weight_copy(PIECES * i, 4).wait()
        for r in OTHERS:
            mix_copy(r, False).wait_send()


VM = pl.BlockSpec(memory_space=pltpu.VMEM)
ANY = pl.BlockSpec(memory_space=pl.ANY)
DMA = pltpu.SemaphoreType.DMA


def line_scratch(n, steps, block, done):
    sems = (2, 2 * n - 2, steps)
    return [pltpu.VMEM((2, n - 1, steps) + block, BF16), pltpu.VMEM((steps,) + done, BF16), DMA(sems), DMA(sems), DMA((steps,))]


def residual_norm(n, xs, bias, gain, mixed, mix_in, o_parts, ship):
    steps, rows, width = xs[0].shape
    out_w = []
    for w in ship:
        half = jax.ShapeDtypeStruct((w.shape[0] // 2, w.shape[1]), BF16)
        out_w += [half, jax.ShapeDtypeStruct(w.shape, BF16), half, half, half]
    done = (8, rows, width // 2)
    far = [mixed, *mix_in, *o_parts, *ship]
    pieces = PIECES * len(ship)
    outs = pl.pallas_call(
        functools.partial(line_body, "norm", len(ship)),
        in_specs=[VM] * 6 + [ANY] * len(far),
        out_specs=[VM, ANY] + [ANY] * len(out_w),
        out_shape=[jax.ShapeDtypeStruct((steps, 4, rows, width), F32), jax.ShapeDtypeStruct((n, steps) + done, BF16)] + out_w,
        scratch_shapes=line_scratch(n, steps, (4, rows, width), done) + [
            DMA((pieces, 5)), DMA((pieces, 5)),
            pltpu.VMEM((n, steps, 4, rows, width), BF16),
            pltpu.VMEM((4, n) + mixed.shape[2:], BF16),
            pltpu.VMEM((4 * width, width), BF16),
            DMA((3,)), DMA((3,)), DMA((11,)),
        ],
        compiler_params=pltpu.CompilerParams(collective_id=0, has_side_effects=True, vmem_limit_bytes=LIMIT),
        cost_estimate=WORK,
        name="residual_norm",
    )(*xs, bias, gain, *far)
    return outs[0], outs[1], [outs[2 + 5 * i:7 + 5 * i] for i in range(len(ship))]


def finish_rows(n, part_a, res, bias, m_all, bias_g, bias_u, pieces):
    steps, _, rows, width = res.shape
    half = steps // 2
    inner_width = bias_g.shape[1]
    toks = n * half * rows
    return pl.pallas_call(
        functools.partial(line_body, "finish", 0),
        in_specs=[ANY, VM, VM, ANY, VM, VM] + [ANY] * len(pieces),
        out_specs=ANY,
        out_shape=jax.ShapeDtypeStruct((n, 4, steps, rows, width), BF16),
        scratch_shapes=line_scratch(n, steps, (4, rows, width), (4, rows, width)) + [
            DMA((3, steps)), DMA((3, steps)),
            pltpu.VMEM((n, steps, 4, rows, width), BF16),
            pltpu.VMEM((n, half) + m_all.shape[2:], BF16),
            pltpu.VMEM((toks, inner_width), BF16),
            pltpu.VMEM((2, 2, 4 * width, TILE), BF16),
            DMA((2,)), DMA((2, 12)),
        ],
        compiler_params=pltpu.CompilerParams(collective_id=1, has_side_effects=True, vmem_limit_bytes=LIMIT),
        cost_estimate=WORK,
        name="finish_rows",
    )(part_a, res, bias, m_all, bias_g, bias_u, *pieces)


def solution(mesh):
    wd_count = mesh.shape['wd']
    ch_count = mesh.shape['ch']
    row_spec = P('dp', 'wd')
    specs = (row_spec, P('dp'), P('wd'), P('wd', 'ch'), P('ch'), P('wd', 'ch'), P('ch'), P(None, 'ch'), P('ch'), P('ch'), P('ch'), P('ch'), P('ch'), P('ch'), P('ch', 'wd'), P('wd'), P('wd'), P('wd', 'ch'), P('ch'), P('wd', 'ch'), P('ch'), P('ch', 'wd'), P('wd'))
    core_hop, y_hop, both_hop = (flip_pairs(wd_count, r) for r in OTHERS)

    def local_layer(resid_in, seg_pos, gain_temporal, w_x, bias_x, w_y, bias_y, conv_w, conv_bias, lam_param, rgate_w, rgate_b, igate_w, igate_b, w_o, bias_o, gain_mlp, w_g, bias_g, w_u, bias_u, w_d, bias_d):
        me, z, dp = lax.axis_index('wd'), lax.axis_index('ch'), lax.axis_index('dp')
        idx = jnp.stack([me, dp, z]).astype(jnp.int32)
        tokens, local_width = resid_in.shape
        model_width = local_width * wd_count
        chunk = tokens // CHUNKS
        share = tokens // (ch_count * wd_count)
        rows = share // SUB
        channels = w_x.shape[1] // wd_count

        def half_from_y(w):
            half = w.shape[0] // 2
            part = lax.dynamic_slice_in_dim(w, dp * half, half, 0)
            return lax.ppermute(part, 'wd', y_hop)

        def gathered(w):
            far_a = half_from_y(w)
            far_b = lax.ppermute(far_a, 'dp', flip_pairs(2, 1))
            core = lax.ppermute(w, 'wd', core_hop)
            both_a = lax.ppermute(far_a, 'wd', core_hop)
            both_b = lax.ppermute(far_b, 'wd', core_hop)
            return w, core, far_a, far_b, both_a, both_b

        vecs = jnp.stack([bias_o, gain_mlp, bias_d])
        vecs = [vecs] + [lax.ppermute(vecs, 'wd', hop) for hop in (core_hop, y_hop, both_hop)]
        vecs = jnp.stack(vecs).astype(F32)[:, :, None, :]
        bias_o_r, gain_r, bias_d_r = vecs[:, 0], vecs[:, 1], vecs[:, 2]

        blocks = resid_in.reshape(ch_count, wd_count, share, local_width)
        line = lax.dynamic_index_in_dim(blocks, z, 0, keepdims=False)
        x_rows = [lax.dynamic_index_in_dim(line, me ^ r, 0, keepdims=False) for r in range(4)]
        early = []
        for r, hop in zip(OTHERS, (core_hop, y_hop, both_hop)):
            early.append(lax.ppermute(x_rows[r], 'wd', hop))
        x_rows = [x_rows[0]] + early

        resid32 = resid_in.astype(F32)
        sum_sq = lax.psum(jnp.sum(resid32 * resid32, axis=1, keepdims=True), 'wd')
        normed = (resid32 * lax.rsqrt(sum_sq / model_width + EPS) * (1.0 + gain_temporal.astype(F32))).astype(BF16)

        cols = lambda arr, r: lax.dynamic_slice_in_dim(arr, (me ^ r) * channels, channels, arr.ndim - 1)
        wxy = [jnp.concatenate([cols(w_x, r), cols(w_y, r)], axis=1) for r in range(4)]
        w_send = jnp.concatenate([wxy[1], wxy[3]], axis=1)
        mine = lambda arr: cols(arr.astype(F32)[None], 0)
        bias_xy = jnp.concatenate([mine(bias_x), mine(bias_y)], axis=1)
        conv = jnp.concatenate([cols(conv_w.astype(F32), 0), mine(conv_bias), jnp.zeros((3, channels), F32)], axis=0)
        soft = jax.nn.softplus(-mine(lam_param))
        block = lambda arr: lax.dynamic_index_in_dim(arr, me, 0, keepdims=False)
        gate_w = jnp.concatenate([block(rgate_w), block(igate_w)], axis=1)
        gate_b = jnp.concatenate([mine(rgate_b), mine(igate_b)], axis=1)
        pos = seg_pos.reshape(tokens, 1)

        w_o_parts = gathered(w_o)

        tail = jnp.zeros((GROUP, channels), F32)
        carry = jnp.zeros((GROUP, channels), F32)
        for k in range(CHUNKS):
            n = lax.slice_in_dim(normed, k * chunk, (k + 1) * chunk, axis=0)
            sent = dot32(n, w_send).astype(BF16)
            sent = lax.ppermute(sent, 'wd', core_hop)
            far = (dot32(n, wxy[2]) + sent[:, 2 * channels:].astype(F32)).astype(BF16)
            far = lax.ppermute(far, 'wd', y_hop)
            own = dot32(n, wxy[0]).astype(BF16)
            mixed, tail, carry = lru(idx, own, sent, far, pos[k * chunk:(k + 1) * chunk], bias_xy, conv, soft, gate_w, gate_b, tail, carry, share)
            if k == 0:
                mix_in = [mixed[0]] + [lax.ppermute(mixed[r], 'wd', hop) for r, hop in zip(OTHERS, (core_hop, y_hop, both_hop))]
        x_rows = [x.reshape(SUB, rows, local_width) for x in x_rows]
        res, m, got = residual_norm(ch_count, x_rows, bias_o_r, gain_r, mixed, mix_in, w_o_parts, [w_g, w_u, w_d])
        g_parts, u_parts, d_parts = ([w, core, far_a, far_b, both_a, both_b] for w, (far_a, core, both_a, far_b, both_b) in zip((w_g, w_u, w_d), got))
        bias_gu = [b.astype(F32)[None] for b in (bias_g, bias_u)]
        inner = gate_up(idx, m, g_parts, u_parts, *bias_gu, TILE)
        d_part = partial_rows(down_body, idx, inner, d_parts, (ch_count, SUB // 2, rows), TILE)
        return finish_rows(ch_count, d_part, res, bias_d_r, m, *bias_gu, g_parts + u_parts + d_parts).reshape(tokens, local_width)

    return jax.shard_map(local_layer, mesh=mesh, in_specs=specs, out_specs=row_spec, check_vma=False)
```

time: 2880 us -> 787 us (0.27)
  waiting for transfers between devices: 1520 us -> 106 us
  local copies, waits for them, and re-layouts: 815 us -> 20.7 us
  Pallas kernels: 0 us -> 582 us
  other arithmetic: 274 us -> 17.9 us
  matrix products: 174 us -> 33.6 us
  starting transfers between devices: 41.6 us -> 12.8 us
    all_to_all x6 -> x0, waiting for transfers between devices: 1070 us -> none  [token_sum(): received = lax.all_to_all(pieces, axis_name, 0, 0)]
    pallas_call x0 -> x6, Pallas kernels: none -> 582 us  [the longest x1 263 us: residual_norm(): pl.pallas_call(functools.partial(line_body, 'norm', len(ship)), in_specs=...]
    slice x78 -> x3, local copies, waits for them, and re-layouts: 512 us -> 2.7 us  [local_layer(): pos[k * chunk:(k + 1) * chunk]]
    all_gather x5 -> x0, waiting for transfers between devices: 449 us -> none  [the longest x1 153 us: local_layer(): inner = lax.all_gather(inner_rows, 'wd', axis=0, tiled=True)]
    pad x22 -> x0, local copies, waits for them, and re-layouts: 230 us -> none  [rg_lru(): lax.associative_scan(combine, (decay.reshape(seqs, steps, width), drive.r...]
    dot_general x8 -> x6, matrix products: 174 us -> 33.6 us  [dot32(): return jnp.dot(a, b, preferred_element_type=F32)]
    ppermute x0 -> x18, waiting for transfers between devices: none -> 106 us  [the longest x3 97.6 us: local_layer(): lax.ppermute(vecs, 'wd', hop)]
    reduce_sum x7 -> x0, other arithmetic: 57.3 us -> none  [the longest x6 52.5 us: token_sum(): return jnp.sum(received.astype(jnp.float32), axis=0)]
  transfers between devices with their start and end apart: 11 -> 18, of which waited for: 9 -> 4; matrix products, arithmetic and copies ran while one was open for 38% -> 6% of each run, Pallas kernels for 0% -> 4%
where the time goes in v1:
time: 787 us; the launch traced here: 786 us
  Pallas kernels  582 us (74%)
  waiting for transfers between devices  106 us (13%)
  matrix products  33.6 us (4%)
  local copies, waits for them, and re-layouts  20.7 us (3%)
  other arithmetic  17.9 us (2%)
  starting transfers between devices  12.8 us (2%)
  blocking collectives  12.7 us (2%)
    pallas_call x1, Pallas kernels, residual_norm(): pl.pallas_call(functools.partial(line_body, 'norm', len(ship)), in_specs=...  263 us
    pallas_call x1, Pallas kernels, finish_rows(): pl.pallas_call(functools.partial(line_body, 'finish', 0), in_specs=[ANY,...  237 us
    ppermute x3, waiting for transfers between devices, local_layer(): lax.ppermute(vecs, 'wd', hop)  97.6 us
    pallas_call x1, Pallas kernels, gate_up(): pl.pallas_call(gate_up_body, grid_spec=pltpu.PrefetchScalarGridSpec(num_s...  35 us
    dot_general x6, matrix products, dot32(): return jnp.dot(a, b, preferred_element_type=F32)  33.6 us
    pallas_call x2, Pallas kernels, lru(): pl.pallas_call(lru_body, grid_spec=pltpu.PrefetchScalarGridSpec(num_scala...  27.7 us
    pallas_call x1, Pallas kernels, partial_rows(): pl.pallas_call(body, grid_spec=pltpu.PrefetchScalarGridSpec(num_scalar_pr...  20 us
  transfers between devices with their start and end apart: 18, of which 4 were waited for; matrix products, arithmetic and copies ran while one was open for 6% of the time, Pallas kernels for 4%

profile of v1, /device:TPU:0, one launch (start us, length us, event | category | flops | bytes accessed | tf_op | source)
XLA Modules:
  0.0 786.3 jit_solution(17412221339088332844)
XLA Ops:
  0.0 0.7 convert_add_fusion
  0.7 5.1 fusion
  5.8 12.7 %psum.7 = f32[4096,1]{0,1:T(1,128)S(1)} all-reduce(f32[4096,1]{0,1:T(1,128)S(1)} %bitcast.57), channel_id=1, replica_groups=mesh['dp'=2,'ch'=4,'wd'=4] {'wd'}, use_global_device_ids=true, to_apply=%region_1.2 | all-reduce | flops 4096 | bytes 32768 | tf_op jit(solution)/shard_map/psum | solution.py:625
  18.6 5.4 fusion.2
  24.0 0.6 constant_dynamic-slice_fusion.2
  24.6 6.5 convolution_convert_fusion
  31.1 6.5 convolution_convert_fusion.1
  38.6 1.3 constant_dynamic-slice_fusion
  39.9 1.7 collective-permute-start.14
  41.6 2.9 dynamic-slice_bitcast_fusion
  44.5 6.0 fusion.16.own_ref
  50.6 5.3 add_convert_fusion
  56.0 1.2 collective-permute-start.9
  57.1 5.5 add_convert_fusion.1
  62.6 0.9 collective-permute-start.7
  63.7 1.1 collective-permute-done.3
  64.8 1.2 collective-permute-start.5
  66.1 1.6 collective-permute-start.15
  67.7 0.7 fusion.25
  68.7 96.6 %collective-permute-done.5 = bf16[3,1024]{1,0:T(4,128)(2,1)S(1)} collective-permute-done((bf16[3,1024]{1,0:T(4,128)(2,1)S(1)}, bf16[3,1024]{1,0:T(4,128)(2,1)S(1)}, u32[]{:S(2)}, u32[]{:S(2)}) %collective-permute-start.5) | collective-permute-done | bytes 6176 | tf_op jit(solution)/shard_map/ppermute | solution.py:612
  165.3 0.9 collective-permute-start.13
  166.1 0.6 pad_maximum_fusion.18
  166.8 1.7 collective-permute-start.1
  168.5 3.7 fusion.13.own_ref
  172.2 8.5 %collective-permute-done.1 = bf16[256,1024]{1,0:T(8,128)(2,1)S(1)} collective-permute-done((bf16[256,1024]{1,0:T(8,128)(2,1)S(1)}, bf16[256,1024]{1,0:T(8,128)(2,1)S(1)}, u32[]{:S(2)}, u32[]{:S(2)}) %collective-permute-start.1) | collective-permute-done | bytes 524320 | tf_op jit(solution)/shard_map/ppermute | solution.py:621
  180.7 1.4 compare_select_fusion
  182.1 0.6 broadcast_in_dim.30
  182.7 0.6 broadcast_in_dim.31
  183.3 1.4 copy.24.pos_ref
  184.7 1.3 copy.25.pos_ref
  186.1 1.0 dynamic-slice_bitcast_fusion.3
  187.1 0.8 pad_maximum_fusion.13.gate_w_ref
  187.9 0.5 collective-permute-start.17
  188.4 0.7 maximum_maximum_fusion.conv_ref
  189.1 0.6 pad_add_fusion.idx_ref
  189.7 0.6 broadcast_1_tail_ref_carry_ref.2.tail_ref.carry_ref
  190.3 13.9 %lru.2 = (bf16[4,2,256,256]{3,2,1,0:T(8,128)(2,1)}, f32[8,256]{1,0:T(8,128)}, f32[8,256]{1,0:T(8,128)}) custom-call(s32[3]{0:T(128)} %pad_add_fusion.idx_ref, bf16[2048,512]{1,0:T(8,128)(2,1)} %fusion.16.own_ref, bf16[2048,1024]{1,0:T(8,128)(2,1)} %collective-permute-done.8.peer_ref, bf16[2048,512]{1,0:T(8,128)(2,1)} %collective-permute-done.9.far_ref, ...), custom_call_target="tpu_custom_call" | custom-call | flops 2097152000 | bytes 10485760 | tf_op jit(solution)/shard_map/lru/pallas_call | solution.py:101
  204.2 2.0 slice_bitcast_fusion
  206.2 1.7 collective-permute-start.12
  208.3 0.7 fusion.24
  209.0 0.6 copy-done.3
  209.7 13.8 %lru.3 = (bf16[4,2,256,256]{3,2,1,0:T(8,128)(2,1)}, f32[8,256]{1,0:T(8,128)}, f32[8,256]{1,0:T(8,128)}) custom-call(s32[3]{0:T(128)} %pad_add_fusion.idx_ref, bf16[2048,512]{1,0:T(8,128)(2,1)} %fusion.13.own_ref, bf16[2048,1024]{1,0:T(8,128)(2,1)} %collective-permute-done.6.peer_ref, bf16[2048,512]{1,0:T(8,128)(2,1)} %copy-done.3, s32[2048,1]{1,0:T(8,128)} %copy.25.pos_ref, ...), custom_call_target="tpu_custom_call" | custom-call | flops 2097152000 | bytes 10485760 | tf_op jit(solution)/shard_map/lru/pallas_call | solution.py:101
  223.5 0.7 copy-done.22
  224.3 262.7 %residual_norm.1 = (f32[16,4,16,1024]{3,2,1,0:T(8,128)}, bf16[4,16,8,16,512]{4,3,2,1,0:T(8,128)(2,1)}, bf16[512,3072]{1,0:T(8,128)(2,1)}, bf16[1024,3072]{1,0:T(...) custom-call(bf16[16,16,1024]{2,1,0:T(8,128)(2,1)} %bitcast.56, ...), custom_call_target="tpu_custom_call" | custom-call | flops 199999995904 | bytes 20000000 | tf_op jit(solution)/shard_map/residual_norm/pallas_call | solution.py:538
  486.9 35.0 %gate_up.1.inner_ref = bf16[2,512,1536]{2,1,0:T(8,128)(2,1)} custom-call(s32[3]{0:T(128)} %pad_add_fusion.idx_ref, bf16[4,16,8,16,512]{4,3,2,1,0:T(8,128)(2,1)} %get-tuple-element.30.m_ref.refs_3_, bf16[1024,3072]{1,0:T(8,128)(2,1)} %refs_6_.3, bf16[1024,3072]{1,0:T(8,128)(2,1)} %get-tuple-element.31.refs_1_.refs_7_, ...), custom_call_target="tpu_custom_call" | custom-call | flops 25769803776 | bytes 50331648 | tf_op jit(solution)/shard_map/gate_up/pallas_call | solution.py:177
  521.9 20.0 %shard_map.217.refs_0_ = bf16[4,8,4,16,1024]{4,3,2,1,0:T(8,128)(2,1)} custom-call(s32[3]{0:T(128)} %pad_add_fusion.idx_ref, bf16[2,512,1536]{2,1,0:T(8,128)(2,1)} %gate_up.1.inner_ref, bf16[3072,1024]{1,0:T(8,128)(2,1)} %refs_18_.3, bf16[3072,1024]{1,0:T(8,128)(2,1)} %get-tuple-element.41.core.refs_19_, bf16[1536,1024]{1,0:T(8,128)(2,1)} %get-tuple-element.42.far_a.refs_20_, ...), custom_call_target="tpu_custom_call" | custom-call | flops 12884901888 | bytes 25165824 | tf_op jit(solution)/shard_map/pallas_call | solution.py:139
  541.9 236.6 %finish_rows.1 = bf16[4,4,16,16,1024]{4,3,2,1,0:T(8,128)(2,1)} custom-call(bf16[4,8,4,16,1024]{4,3,2,1,0:T(8,128)(2,1)} %shard_map.217.refs_0_, f32[16,4,16,1024]{3,2,1,0:T(8,128)} %get-tuple-element.46.refs_1_, f32[4,1,1024]{2,1,0:T(1,128)} %get-tuple-element.63.refs_2_, bf16[4,16,8,16,512]{4,3,2,1,0:T(8,128)(2,1)} %get-tuple-element.30.m_ref.refs_3_, ...), custom_call_target="tpu_custom_call" | custom-call | flops 199999995904 | bytes 20000000 | tf_op jit(solution)/shard_map/finish_rows/pallas_call | solution.py:562
  778.5 7.8 copy.27
  (89 shorter events, 2.5 us)
Async XLA Ops:
  18.5 5.4 copy-start.1
  18.5 5.4 copy-start.2
  24.0 7.1 copy-start
  24.5 20.0 %copy-start.4 = (bf16[1024,256]{1,0:T(8,128)(2,1)}, bf16[1024,256]{1,0:T(8,128)(2,1)S(1)}, u32[]{:S(2)}) copy-start(bf16[1024,256]{1,0:T(8,128)(2,1)S(1)} %get-tuple-element.57) | copy-start | bytes 1572868
  24.6 19.9 %copy-start.6 = (bf16[1024,256]{1,0:T(8,128)(2,1)}, bf16[1024,256]{1,0:T(8,128)(2,1)S(1)}, u32[]{:S(2)}) copy-start(bf16[1024,256]{1,0:T(8,128)(2,1)S(1)} %get-tuple-element.71) | copy-start | bytes 1572868
  31.1 7.0 copy-start.12
  31.1 7.0 copy-start.13
  31.1 7.0 copy-start.14
  31.1 19.5 %collective-permute-start.8 = (bf16[2048,1024]{1,0:T(8,128)(2,1)}, bf16[2048,1024]{1,0:T(8,128)(2,1)}, u32[]{:S(2)}, u32[]{:S(2)}) collective-permute-start(bf16[2048,1024]{1,0:T(8,128)(2,1)} %convolution_convert_fusion), channel_id=1, source_target_pairs={{0,1},{1,0},{2,3},{3,2},{4,5},{5,4},{6,7},{7,6},{8,9},{9,8},{10,11... | collective-permute-start | bytes 12582920 | tf_op jit(solution)/shard_map/ppermute | solution.py:647
  37.6 19.5 %collective-permute-start.6 = (bf16[2048,1024]{1,0:T(8,128)(2,1)}, bf16[2048,1024]{1,0:T(8,128)(2,1)}, u32[]{:S(2)}, u32[]{:S(2)}) collective-permute-start(bf16[2048,1024]{1,0:T(8,128)(2,1)} %convolution_convert_fusion.1), channel_id=1, source_target_pairs={{0,1},{1,0},{2,3},{3,2},{4,5},{5,4},{6,7},{7,6},{8,9},{9,8},{10,11... | collective-permute-start | bytes 12582920 | tf_op jit(solution)/shard_map/ppermute | solution.py:647
  38.1 25.4 %collective-permute-start.4 = (bf16[3,1024]{1,0:T(4,128)(2,1)S(1)}, bf16[3,1024]{1,0:T(4,128)(2,1)S(1)}, u32[]{:S(2)}, u32[]{:S(2)}) collective-permute-start(bf16[3,1024]{1,0:T(4,128)(2,1)S(1)} %pad_maximum_fusion.17), channel_id=1, source_target_pairs={{0,2},{1,3},{2,0},{3,1},{4,6},{5,7},{6,4},{7,5},{8,10},{9,11},{10,... | collective-permute-start | bytes 18440 | tf_op jit(solution)/shard_map/ppermute | solution.py:612
  39.9 26.2 %collective-permute-start.14 = (bf16[512,1024]{1,0:T(8,128)(2,1)S(1)}, bf16[512,1024]{1,0:T(8,128)(2,1)}, u32[]{:S(2)}, u32[]{:S(2)}) collective-permute-start(bf16[512,1024]{1,0:T(8,128)(2,1)S(1)} %constant_dynamic-slice_fusion), channel_id=1, source_target_pairs={{0,2},{1,3},{2,0},{3,1},{4,6},{5,7},{6,4},{7,5},{8,10},{9,11},{10,... | collective-permute-start | bytes 3145736 | tf_op jit(solution)/shard_map/ppermute | solution.py:601
  41.6 9.0 %slice-start = ((s8[8388608]{0:T(1024)(128)(4,1)}), s8[4194304]{0:T(1024)(128)(4,1)S(1)}, s32[]{:S(2)}) async-start(s8[8388608]{0:T(1024)(128)(4,1)} %bitcast.53), calls=%async_computation | async-start | bytes 8388608
  44.5 122.2 %collective-permute-start.2 = (bf16[256,1024]{1,0:T(8,128)(2,1)S(1)}, bf16[256,1024]{1,0:T(8,128)(2,1)S(1)}, u32[]{:S(2)}, u32[]{:S(2)}) collective-permute-start(bf16[256,1024]{1,0:T(8,128)(2,1)S(1)} %get-tuple-element.47), channel_id=1, source_target_pairs={{0,3},{1,2},{2,1},{3,0},{4,7},{5,6},{6,5},{7,4},{8,11},{9,10},{10,... | collective-permute-start | bytes 1572872 | tf_op jit(solution)/shard_map/ppermute | solution.py:621
  44.5 6.1 slice-start.1
  55.9 7.6 copy-start.9
  55.9 12.5 %copy-start.15 = (bf16[1024]{0:T(1024)(128)(2,1)S(1)}, bf16[1024]{0:T(1024)(128)(2,1)}, u32[]{:S(2)}) copy-start(bf16[1024]{0:T(1024)(128)(2,1)} %param.27) | copy-start | bytes 6148
  55.9 12.5 %copy-start.16 = (bf16[1024]{0:T(1024)(128)(2,1)S(1)}, bf16[1024]{0:T(1024)(128)(2,1)}, u32[]{:S(2)}) copy-start(bf16[1024]{0:T(1024)(128)(2,1)} %param.29) | copy-start | bytes 6148
  55.9 12.6 %copy-start.17 = (bf16[1024]{0:T(1024)(128)(2,1)S(1)}, bf16[1024]{0:T(1024)(128)(2,1)}, u32[]{:S(2)}) copy-start(bf16[1024]{0:T(1024)(128)(2,1)} %param.34) | copy-start | bytes 6148
  55.9 12.7 %copy-start.18 = (bf16[1024]{0:T(1024)(128)(2,1)S(1)}, bf16[1024]{0:T(1024)(128)(2,1)}, u32[]{:S(2)}) copy-start(bf16[1024]{0:T(1024)(128)(2,1)} %param.36) | copy-start | bytes 6148
  55.9 112.5 %copy-start.5 = (bf16[1024,256]{1,0:T(8,128)(2,1)S(1)}, bf16[1024,256]{1,0:T(8,128)(2,1)}, u32[]{:S(2)}) copy-start(bf16[1024,256]{1,0:T(8,128)(2,1)} %copy-done.4) | copy-start | bytes 1572868
  55.9 112.5 %copy-start.7 = (bf16[1024,256]{1,0:T(8,128)(2,1)S(1)}, bf16[1024,256]{1,0:T(8,128)(2,1)}, u32[]{:S(2)}) copy-start(bf16[1024,256]{1,0:T(8,128)(2,1)} %copy-done.6) | copy-start | bytes 1572868
  56.0 133.1 %collective-permute-start.9 = (bf16[2048,512]{1,0:T(8,128)(2,1)}, bf16[2048,512]{1,0:T(8,128)(2,1)}, u32[]{:S(2)}, u32[]{:S(2)}) collective-permute-start(bf16[2048,512]{1,0:T(8,128)(2,1)} %add_convert_fusion), channel_id=1, source_target_pairs={{0,2},{1,3},{2,0},{3,1},{4,6},{5,7},{6,4},{7,5},{8,10},{9,11},{10,... | collective-permute-start | bytes 6291464 | tf_op jit(solution)/shard_map/ppermute | solution.py:649
  62.6 145.7 %collective-permute-start.7 = (bf16[2048,512]{1,0:T(8,128)(2,1)}, bf16[2048,512]{1,0:T(8,128)(2,1)S(1)}, u32[]{:S(2)}, u32[]{:S(2)}) collective-permute-start(bf16[2048,512]{1,0:T(8,128)(2,1)} %add_convert_fusion.1), channel_id=1, source_target_pairs={{0,2},{1,3},{2,0},{3,1},{4,6},{5,7},{6,4},{7,5},{8,10},{9,11},{10,... | collective-permute-start | bytes 6291464 | tf_op jit(solution)/shard_map/ppermute | solution.py:649
  63.5 1.2 collective-permute-start.3
  64.8 100.5 %collective-permute-start.5 = (bf16[3,1024]{1,0:T(4,128)(2,1)S(1)}, bf16[3,1024]{1,0:T(4,128)(2,1)S(1)}, u32[]{:S(2)}, u32[]{:S(2)}) collective-permute-start(bf16[3,1024]{1,0:T(4,128)(2,1)S(1)} %pad_maximum_fusion.17), channel_id=1, source_target_pairs={{0,3},{1,2},{2,1},{3,0},{4,7},{5,6},{6,5},{7,4},{8,11},{9,10},{10,... | collective-permute-start | bytes 18440 | tf_op jit(solution)/shard_map/ppermute | solution.py:612
  66.1 121.8 %collective-permute-start.15 = (bf16[512,1024]{1,0:T(8,128)(2,1)}, bf16[512,1024]{1,0:T(8,128)(2,1)}, u32[]{:S(2)}, u32[]{:S(2)}) collective-permute-start(bf16[512,1024]{1,0:T(8,128)(2,1)} %collective-permute-done.14.refs_13_), channel_id=1, source_target_pairs={{0,16},{16,0},{1,17},{17,1},{2,18},{18,2},{3,19},{19,3},{4,20},{20... | collective-permute-start | bytes 3145736 | tf_op jit(solution)/shard_map/ppermute | solution.py:605
  165.3 58.2 %collective-permute-start.13 = (bf16[1024,1024]{1,0:T(8,128)(2,1)}, bf16[1024,1024]{1,0:T(8,128)(2,1)}, u32[]{:S(2)}, u32[]{:S(2)}) collective-permute-start(bf16[1024,1024]{1,0:T(8,128)(2,1)} %refs_11_.1), channel_id=1, source_target_pairs={{0,1},{1,0},{2,3},{3,2},{4,5},{5,4},{6,7},{7,6},{8,9},{9,8},{10,11... | collective-permute-start | bytes 6291464 | tf_op jit(solution)/shard_map/ppermute | solution.py:606
  166.7 5.5 copy-start.20
  166.7 15.3 %copy-start.19 = (bf16[1024]{0:T(1024)(128)(2,1)S(1)}, bf16[1024]{0:T(1024)(128)(2,1)}, u32[]{:S(2)}) copy-start(bf16[1024]{0:T(1024)(128)(2,1)} %param.31) | copy-start | bytes 6148
  166.7 15.4 %copy-start.10 = (bf16[3072]{0:T(1024)(128)(2,1)S(1)}, bf16[3072]{0:T(1024)(128)(2,1)}, u32[]{:S(2)}) copy-start(bf16[3072]{0:T(1024)(128)(2,1)} %param.41) | copy-start | bytes 18436
  166.8 16.0 %copy-start.11 = (bf16[3072]{0:T(1024)(128)(2,1)S(1)}, bf16[3072]{0:T(1024)(128)(2,1)}, u32[]{:S(2)}) copy-start(bf16[3072]{0:T(1024)(128)(2,1)} %param.43) | copy-start | bytes 18436
  166.8 22.3 %copy-start.8 = (bf16[256,1024]{1,0:T(8,128)(2,1)S(1)}, bf16[256,1024]{1,0:T(8,128)(2,1)}, u32[]{:S(2)}) copy-start(bf16[256,1024]{1,0:T(8,128)(2,1)} %get-tuple-element.49) | copy-start | bytes 1572868
  166.8 13.9 %collective-permute-start.1 = (bf16[256,1024]{1,0:T(8,128)(2,1)S(1)}, bf16[256,1024]{1,0:T(8,128)(2,1)S(1)}, u32[]{:S(2)}, u32[]{:S(2)}) collective-permute-start(bf16[256,1024]{1,0:T(8,128)(2,1)S(1)} %get-tuple-element.48), channel_id=1, source_target_pairs={{0,2},{1,3},{2,0},{3,1},{4,6},{5,7},{6,4},{7,5},{8,10},{9,11},{10,... | collective-permute-start | bytes 1572872 | tf_op jit(solution)/shard_map/ppermute | solution.py:621
  180.7 23.5 %copy-start.21 = (bf16[256,1024]{1,0:T(8,128)(2,1)}, bf16[256,1024]{1,0:T(8,128)(2,1)S(1)}, u32[]{:S(2)}) copy-start(bf16[256,1024]{1,0:T(8,128)(2,1)S(1)} %collective-permute-done.1) | copy-start | bytes 1572868
  180.7 27.2 %collective-permute-start.16 = (bf16[512,1024]{1,0:T(8,128)(2,1)}, bf16[512,1024]{1,0:T(8,128)(2,1)}, u32[]{:S(2)}, u32[]{:S(2)}) collective-permute-start(bf16[512,1024]{1,0:T(8,128)(2,1)} %collective-permute-done.14.refs_13_), channel_id=1, source_target_pairs={{0,1},{1,0},{2,3},{3,2},{4,5},{5,4},{6,7},{7,6},{8,9},{9,8},{10,11... | collective-permute-start | bytes 3145736 | tf_op jit(solution)/shard_map/ppermute | solution.py:607
  187.9 35.6 %collective-permute-start.17 = (bf16[512,1024]{1,0:T(8,128)(2,1)}, bf16[512,1024]{1,0:T(8,128)(2,1)}, u32[]{:S(2)}, u32[]{:S(2)}) collective-permute-start(bf16[512,1024]{1,0:T(8,128)(2,1)} %collective-permute-done.15.refs_14_), channel_id=1, source_target_pairs={{0,1},{1,0},{2,3},{3,2},{4,5},{5,4},{6,7},{7,6},{8,9},{9,8},{10,11... | collective-permute-start | bytes 3145736 | tf_op jit(solution)/shard_map/ppermute | solution.py:608
  189.0 17.1 %collective-permute-start = (bf16[256,1024]{1,0:T(8,128)(2,1)S(1)}, bf16[256,1024]{1,0:T(8,128)(2,1)}, u32[]{:S(2)}, u32[]{:S(2)}) collective-permute-start(bf16[256,1024]{1,0:T(8,128)(2,1)S(1)} %copy-done.8), channel_id=1, source_target_pairs={{0,1},{1,0},{2,3},{3,2},{4,5},{5,4},{6,7},{7,6},{8,9},{9,8},{10,11... | collective-permute-start | bytes 1572872 | tf_op jit(solution)/shard_map/ppermute | solution.py:621
  206.2 17.3 %collective-permute-start.12 = (bf16[2,256,256]{2,1,0:T(8,128)(2,1)S(1)}, bf16[2,256,256]{2,1,0:T(8,128)(2,1)S(1)}, u32[]{:S(2)}, u32[]{:S(2)}) collective-permute-start(bf16[2,256,256]{2,1,0:T(8,128)(2,1)S(1)} %get-tuple-element.59), channel_id=1, source_target_pairs={{0,3},{1,2},{2,1},{3,0},{4,7},{5,6},{6,5},{7,4},{8,11},{9,10},{10,... | collective-permute-start | bytes 786440 | tf_op jit(solution)/shard_map/ppermute | solution.py:653
  207.9 15.6 %collective-permute-start.11 = (bf16[2,256,256]{2,1,0:T(8,128)(2,1)S(1)}, bf16[2,256,256]{2,1,0:T(8,128)(2,1)S(1)}, u32[]{:S(2)}, u32[]{:S(2)}) collective-permute-start(bf16[2,256,256]{2,1,0:T(8,128)(2,1)S(1)} %get-tuple-element.60), channel_id=1, source_target_pairs={{0,2},{1,3},{2,0},{3,1},{4,6},{5,7},{6,4},{7,5},{8,10},{9,11},{10,... | collective-permute-start | bytes 786440 | tf_op jit(solution)/shard_map/ppermute | solution.py:653
  208.3 1.4 copy-start.3
  208.3 15.2 %collective-permute-start.10 = (bf16[2,256,256]{2,1,0:T(8,128)(2,1)S(1)}, bf16[2,256,256]{2,1,0:T(8,128)(2,1)}, u32[]{:S(2)}, u32[]{:S(2)}) collective-permute-start(bf16[2,256,256]{2,1,0:T(8,128)(2,1)S(1)} %get-tuple-element.61), channel_id=1, source_target_pairs={{0,1},{1,0},{2,3},{3,2},{4,5},{5,4},{6,7},{7,6},{8,9},{9,8},{10,11... | collective-permute-start | bytes 786440 | tf_op jit(solution)/shard_map/ppermute | solution.py:653
  223.5 0.7 copy-start.22
  223.5 0.8 copy-start.23

commit v2 on v1

--- a/solution.py
+++ b/solution.py
@@ -9,9 +9,9 @@
 
 
 EPS = 1e-6
-CHUNKS = 2
+SPLIT = (3, 1)
 SUB = 16
-TILE = 256
+TILE = 512
 PIECES = 4
 GROUP = 8
 WAYS = (0, 1)
@@ -114,81 +114,6 @@
     )(idx, own, peer, far, pos, bias, conv, sp, gate_w, gate_b, tail, carry)
 
 
-def pieces_specs(pieces, cols):
-    return [pl.BlockSpec((w.shape[0], cols), lambda j, idx: (0, j)) for w in pieces]
-
-
-def put_rows(out_ref, r, val):
-    zs, steps, _, rows, cols = out_ref.shape
-    out_ref[:, :, r] = val.astype(BF16).reshape(zs, steps, rows, cols)
-
-
-def down_body(idx_ref, inner_ref, own, core, far_a, far_b, both_a, both_b, out_ref):
-    dp = idx_ref[1]
-    half = inner_ref.shape[2]
-    put = functools.partial(put_rows, out_ref)
-    for r, w in ((0, own), (1, core)):
-        put(r, dot32(inner_ref[0], w[0:half, :]) + dot32(inner_ref[1], w[half:2 * half, :]))
-    for r, near, far in ((2, far_a, far_b), (3, both_a, both_b)):
-        put(r, dot32(inner_ref[dp], near[...]) + dot32(inner_ref[1 - dp], far[...]))
-
-
-def partial_rows(body, idx, lhs, pieces, grid_rows, cols):
-    zs, steps, rows = grid_rows
-    depth, width = pieces[0].shape
-    return pl.pallas_call(
-        body,
-        grid_spec=pltpu.PrefetchScalarGridSpec(
-            num_scalar_prefetch=1,
-            grid=(width // cols,),
-            in_specs=[pl.BlockSpec(lhs.shape, lambda j, idx: (0,) * lhs.ndim)] + pieces_specs(pieces, cols),
-            out_specs=pl.BlockSpec((zs, steps, 4, rows, cols), lambda j, idx: (0, 0, 0, 0, j)),
-        ),
-        out_shape=jax.ShapeDtypeStruct((zs, steps, 4, rows, width), BF16),
-        compiler_params=pltpu.CompilerParams(dimension_semantics=("arbitrary",)),
-        cost_estimate=pl.CostEstimate(flops=2 * zs * steps * rows * depth * 4 * width, bytes_accessed=depth * 4 * width * 2, transcendentals=0),
-    )(idx, lhs, *pieces)
-
-
-def gate_up_body(idx_ref, m_ref, *refs):
-    dp = idx_ref[1]
-    g_parts, u_parts, (bias_g, bias_u, inner_ref) = refs[:6], refs[6:12], refs[12:]
-    zs, steps, _, rows, depth = m_ref.shape
-    lhs = lambda k: m_ref[:, :, k].reshape(zs * steps * rows, depth)
-
-    def product(parts):
-        own, core, far_a, far_b, both_a, both_b = parts
-        acc = dot32(lhs(0), own[0:depth, :]) + dot32(lhs(1), own[depth:2 * depth, :])
-        acc = acc + dot32(lhs(2), core[0:depth, :]) + dot32(lhs(3), core[depth:2 * depth, :])
-        acc = acc + dot32(lhs(4 + dp), far_a[...]) + dot32(lhs(5 - dp), far_b[...])
-        return acc + dot32(lhs(6 + dp), both_a[...]) + dot32(lhs(7 - dp), both_b[...])
-
-    gate = jax.nn.gelu(product(g_parts) + bias_g[...], approximate=True)
-    inner_ref[0] = (gate * (product(u_parts) + bias_u[...])).astype(BF16)
-
-
-def gate_up(idx, m, g_pieces, u_pieces, bias_g, bias_u, cols):
-    zs, steps, ks, rows, depth = m.shape
-    steps = steps // 2
-    toks = zs * steps * rows
-    width = g_pieces[0].shape[1]
-    tiles = width // cols
-    bias_spec = pl.BlockSpec((1, cols), lambda j, idx: (0, j))
-    return pl.pallas_call(
-        gate_up_body,
-        grid_spec=pltpu.PrefetchScalarGridSpec(
-            num_scalar_prefetch=1,
-            grid=(tiles,),
-            in_specs=[pl.BlockSpec((zs, steps, ks, rows, depth), lambda j, idx: (0,) * 5)] + pieces_specs(g_pieces, cols) + pieces_specs(u_pieces, cols) + [bias_spec, bias_spec],
-            out_specs=pl.BlockSpec((1, toks, cols), lambda j, idx: (j // (tiles // 2), 0, j % (tiles // 2))),
-        ),
-        out_shape=jax.ShapeDtypeStruct((2, toks, width // 2), BF16),
-        compiler_params=pltpu.CompilerParams(dimension_semantics=("arbitrary",)),
-        cost_estimate=pl.CostEstimate(flops=4 * toks * ks * depth * width, bytes_accessed=4 * ks * depth * width, transcendentals=toks * width),
-        name="gate_up",
-    )(idx, m, *g_pieces, *u_pieces, bias_g, bias_u)
-
-
 def line_body(kind, n_ship, *refs):
     if kind == "norm":
         x_rows, (bias, gain, mixed), mix_in, o_parts = refs[:4], refs[4:7], refs[7:11], refs[11:17]
@@ -197,15 +122,15 @@
         shipped, refs = refs[2:2 + 5 * n_ship], refs[2 + 5 * n_ship:]
         rbuf, obuf, send, recv, loc, w_send, w_recv, part, mixbuf, wo, a_send, a_recv, pre_sem = refs
     else:
-        part_a, res_ref, bias, m_all, bias_g, bias_u = refs[:6]
-        g_parts, u_parts, d_parts = refs[6:12], refs[12:18], refs[18:24]
-        out, rbuf, obuf, send, recv, loc, a_send, a_recv, part, mbuf, inner, wbuf, pre_sem, tile_sem = refs[24:]
+        res_ref, bias, m_all, bias_g, bias_u = refs[:5]
+        g_parts, u_parts, d_parts = refs[5:11], refs[11:17], refs[17:23]
+        out, late_b, late_both, rbuf, obuf, send, recv, loc, a_send, a_recv, part, mbuf, inner, wbuf, pre_sem, tile_sem, l_send, l_recv = refs[23:]
     n = rbuf.shape[1] + 1
     steps = rbuf.shape[2]
     z, me, dp = lax.axis_index('ch'), lax.axis_index('wd'), lax.axis_index('dp')
     lag = 0 if kind == "norm" else 1
     wd_to = lambda r: {'wd': me ^ r}
-    peers = [wd_to(r) for r in OTHERS] + ([{'dp': 1 - dp}] if kind == "norm" else [])
+    peers = [wd_to(r) for r in OTHERS] + [{'dp': 1 - dp}]
 
     barrier = pltpu.get_barrier_semaphore()
     for peer in peers:
@@ -316,12 +241,13 @@
             mix_copy(r, True).wait_recv()
         lax.fori_loop(first, 4 * n, project, 0)
 
+    crossed = PIECES * n_ship - PIECES // 2
     half = steps // 2
     if kind != "norm":
         gates = inner.shape[1] // TILE
         per_block = part.shape[4] // TILE
         tiles = gates + 4 * per_block
-        loads = [pltpu.make_async_copy(part_a, part.at[:, pl.ds(0, half)], pre_sem.at[0]), pltpu.make_async_copy(m_all.at[:, pl.ds(half, half)], mbuf, pre_sem.at[1])]
+        loads = [pltpu.make_async_copy(m_all.at[:, pl.ds(i * half, half)], mbuf.at[i], pre_sem.at[i]) for i in WAYS]
 
         def tile_copies(q, down_block):
             slot = lax.rem(q, 2)
@@ -333,7 +259,8 @@
                 own, core, far_a, far_b, both_a, both_b = d_parts
                 rows_a = dp * far_a.shape[0]
                 rows_b = far_a.shape[0] - rows_a
-                jobs = ([(own, 0, 0)], [(core, 0, 0)], [(far_a, 0, rows_a), (far_b, 0, rows_b)], [(both_a, 0, rows_a), (both_b, 0, rows_b)])[down_block]
+                late = rows_b + far_b.shape[0]
+                jobs = ([(own, 0, 0)], [(core, 0, 0)], [(far_a, 0, rows_a), (far_b, 0, rows_b), (late_b, 0, late)], [(both_a, 0, rows_a), (both_b, 0, rows_b), (late_both, 0, late)])[down_block]
             return [pltpu.make_async_copy(w.at[:, at], wbuf.at[slot, i, pl.ds(to, w.shape[0]), :], tile_sem.at[slot, j]) for j, (w, i, to) in enumerate(jobs)]
 
         def for_tile(q, act):
@@ -348,9 +275,31 @@
                     for copy in tile_copies(q, r):
                         act(copy)
 
-        def mlp_tile(q, _):
+        def late_copy(j):
+            far_a, size = d_parts[2], late_b.shape[0]
+            src, dst, to = ((far_a.at[pl.ds(size, size)], late_b, {'dp': 1 - dp}), (late_b, late_both, wd_to(1)))[j]
+            return pltpu.make_async_remote_copy(src_ref=src, dst_ref=dst, send_sem=l_send.at[j], recv_sem=l_recv.at[j], device_id=to, device_id_type=MESH)
+
+        late_copy(0).start()
+
+        def mlp_tile(job, _):
+            phase, q = lax.div(job, tiles), lax.rem(job, tiles)
+
+            @pl.when(job == gates + per_block)
+            def _():
+                late_copy(0).wait_recv()
+                late_copy(1).start()
+
+            @pl.when(job == gates + 3 * per_block - 1)
+            def _():
+                late_copy(1).wait_recv()
+
             for_tile(q, lambda copy: copy.wait())
-            for_tile(q + 1, lambda copy: copy.start())
+
+            @pl.when(job < 2 * tiles - 1)
+            def _():
+                for_tile(lax.rem(job + 1, tiles), lambda copy: copy.start())
+
             slot = lax.rem(q, 2)
             toks = inner.shape[0]
 
@@ -359,12 +308,7 @@
                 at = pl.ds(pl.multiple_of(q * TILE, TILE), TILE)
                 sums = []
                 for i in range(2):
-                    acc = None
-                    depth = mbuf.shape[4]
-                    for k in range(mbuf.shape[2]):
-                        val = dot32(mbuf[:, :, k].reshape(toks, depth), wbuf[slot, i, k * depth:(k + 1) * depth, :])
-                        acc = val if acc is None else acc + val
-                    sums.append(acc)
+                    sums.append(dot32(mbuf[phase].reshape(toks, mbuf.shape[4]), wbuf[slot, i]))
                 gate = jax.nn.gelu(sums[0] + bias_g[:, at], approximate=True)
                 inner[:, at] = (gate * (sums[1] + bias_u[:, at])).astype(BF16)
 
@@ -373,15 +317,16 @@
                 d = q - gates
                 at = pl.ds(pl.multiple_of(lax.rem(d, per_block) * TILE, TILE), TILE)
                 val = dot32(inner[...], wbuf[slot, 0, 0:inner.shape[1], :]).astype(BF16)
-                part[:, pl.ds(half, half), lax.div(d, per_block), :, at] = val.reshape(n, half, part.shape[3], TILE)
+                part[:, pl.ds(phase * half, half), lax.div(d, per_block), :, at] = val.reshape(n, half, part.shape[3], TILE)
 
             return 0
 
         for copy in loads:
             copy.start()
         for_tile(0 * z, lambda copy: copy.start())
-        for copy in loads:
-            copy.wait()
+        loads[0].wait()
+        lax.fori_loop(0, tiles, mlp_tile, 0)
+        loads[1].wait()
 
     def finish(s):
         for way in WAYS:
@@ -407,8 +352,7 @@
             scale = lax.rsqrt(total / (4 * width) + EPS)
             for r in BLOCKS:
                 normed = (res_ref[s, r] * scale * (1.0 + gain[r])).astype(BF16)
-                obuf[s, 2 * r] = normed[:, :width // 2]
-                obuf[s, 2 * r + 1] = normed[:, width // 2:]
+                obuf[s, :, r * width:(r + 1) * width] = normed
         else:
             for r in OTHERS:
                 swap(r, s).start()
@@ -467,23 +411,25 @@
         if kind != "norm":
             @pl.when(t < half)
             def _():
-                lax.fori_loop(lax.div(t * tiles, half), lax.div((t + 1) * tiles, half), mlp_tile, 0)
+                lax.fori_loop(tiles + lax.div(t * tiles, half), tiles + lax.div((t + 1) * tiles, half), mlp_tile, 0)
 
         if kind == "norm":
             for q in range(PIECES * n_ship):
-                @pl.when(t == (3 * q + 9) // 2)
+                @pl.when(t == (3 * q + 5) // 2)
                 def _(q=q):
                     weight_copy(q, 0).wait_recv()
-                    weight_copy(q, 1).start()
+                    if q < crossed:
+                        weight_copy(q, 1).start()
                     weight_copy(q, 2).start()
 
-                @pl.when(t == (3 * q + 14) // 2)
-                def _(q=q):
-                    weight_copy(q, 1).wait_recv()
-                    weight_copy(q, 3).start()
+                if q < crossed:
+                    @pl.when(t == (3 * q + 10) // 2)
+                    def _(q=q):
+                        weight_copy(q, 1).wait_recv()
+                        weight_copy(q, 3).start()
         return 0
 
-    lax.fori_loop(0, steps + 2 * n, step, 0)
+    lax.fori_loop(0, steps + 2 * n - 2 + lag, step, 0)
 
     def drain(s, _):
         for way in WAYS:
@@ -503,13 +449,18 @@
                 swap(r, s).wait_send()
         return 0
 
+    if kind != "norm":
+        for j in WAYS:
+            late_copy(j).wait_send()
+
     lax.fori_loop(0, steps, drain, 0)
     if kind == "norm":
         for q in range(PIECES * n_ship):
             weight_copy(q, 0).wait_send()
             weight_copy(q, 2).wait()
-            weight_copy(q, 1).wait_send()
-            weight_copy(q, 3).wait()
+            if q < crossed:
+                weight_copy(q, 1).wait_send()
+                weight_copy(q, 3).wait()
         for i in range(n_ship):
             weight_copy(PIECES * i, 4).wait()
         for r in OTHERS:
@@ -531,8 +482,12 @@
     out_w = []
     for w in ship:
         half = jax.ShapeDtypeStruct((w.shape[0] // 2, w.shape[1]), BF16)
-        out_w += [half, jax.ShapeDtypeStruct(w.shape, BF16), half, half, half]
-    done = (8, rows, width // 2)
+        if w is ship[-1]:
+            late = jax.ShapeDtypeStruct((w.shape[0] // 4, w.shape[1]), BF16)
+        else:
+            late = half
+        out_w += [half, jax.ShapeDtypeStruct(w.shape, BF16), half, late, late]
+    done = (rows, 4 * width)
     far = [mixed, *mix_in, *o_parts, *ship]
     pieces = PIECES * len(ship)
     outs = pl.pallas_call(
@@ -554,28 +509,28 @@
     return outs[0], outs[1], [outs[2 + 5 * i:7 + 5 * i] for i in range(len(ship))]
 
 
-def finish_rows(n, part_a, res, bias, m_all, bias_g, bias_u, pieces):
+def finish_rows(n, res, bias, m_all, bias_g, bias_u, pieces):
     steps, _, rows, width = res.shape
     half = steps // 2
     inner_width = bias_g.shape[1]
     toks = n * half * rows
     return pl.pallas_call(
         functools.partial(line_body, "finish", 0),
-        in_specs=[ANY, VM, VM, ANY, VM, VM] + [ANY] * len(pieces),
-        out_specs=ANY,
-        out_shape=jax.ShapeDtypeStruct((n, 4, steps, rows, width), BF16),
+        in_specs=[VM, VM, ANY, VM, VM] + [ANY] * len(pieces),
+        out_specs=[ANY] * 3,
+        out_shape=[jax.ShapeDtypeStruct((n, 4, steps, rows, width), BF16)] + [jax.ShapeDtypeStruct(pieces[-1].shape, BF16)] * 2,
         scratch_shapes=line_scratch(n, steps, (4, rows, width), (4, rows, width)) + [
             DMA((3, steps)), DMA((3, steps)),
             pltpu.VMEM((n, steps, 4, rows, width), BF16),
-            pltpu.VMEM((n, half) + m_all.shape[2:], BF16),
+            pltpu.VMEM((2, n, half) + m_all.shape[2:], BF16),
             pltpu.VMEM((toks, inner_width), BF16),
             pltpu.VMEM((2, 2, 4 * width, TILE), BF16),
-            DMA((2,)), DMA((2, 12)),
+            DMA((2,)), DMA((2, 12)), DMA((2,)), DMA((2,)),
         ],
         compiler_params=pltpu.CompilerParams(collective_id=1, has_side_effects=True, vmem_limit_bytes=LIMIT),
         cost_estimate=WORK,
         name="finish_rows",
-    )(part_a, res, bias, m_all, bias_g, bias_u, *pieces)
+    )(res, bias, m_all, bias_g, bias_u, *pieces)[0]
 
 
 def solution(mesh):
@@ -590,7 +545,7 @@
         idx = jnp.stack([me, dp, z]).astype(jnp.int32)
         tokens, local_width = resid_in.shape
         model_width = local_width * wd_count
-        chunk = tokens // CHUNKS
+        unit = tokens // sum(SPLIT)
         share = tokens // (ch_count * wd_count)
         rows = share // SUB
         channels = w_x.shape[1] // wd_count
@@ -641,22 +596,21 @@
 
         tail = jnp.zeros((GROUP, channels), F32)
         carry = jnp.zeros((GROUP, channels), F32)
-        for k in range(CHUNKS):
-            n = lax.slice_in_dim(normed, k * chunk, (k + 1) * chunk, axis=0)
+        for k, size in enumerate(SPLIT):
+            start, stop = sum(SPLIT[:k]) * unit, sum(SPLIT[:k + 1]) * unit
+            n = lax.slice_in_dim(normed, start, stop, axis=0)
             sent = dot32(n, w_send).astype(BF16)
             sent = lax.ppermute(sent, 'wd', core_hop)
             far = (dot32(n, wxy[2]) + sent[:, 2 * channels:].astype(F32)).astype(BF16)
             far = lax.ppermute(far, 'wd', y_hop)
             own = dot32(n, wxy[0]).astype(BF16)
-            mixed, tail, carry = lru(idx, own, sent, far, pos[k * chunk:(k + 1) * chunk], bias_xy, conv, soft, gate_w, gate_b, tail, carry, share)
+            mixed, tail, carry = lru(idx, own, sent, far, pos[start:stop], bias_xy, conv, soft, gate_w, gate_b, tail, carry, share)
             if k == 0:
                 mix_in = [mixed[0]] + [lax.ppermute(mixed[r], 'wd', hop) for r, hop in zip(OTHERS, (core_hop, y_hop, both_hop))]
         x_rows = [x.reshape(SUB, rows, local_width) for x in x_rows]
         res, m, got = residual_norm(ch_count, x_rows, bias_o_r, gain_r, mixed, mix_in, w_o_parts, [w_g, w_u, w_d])
         g_parts, u_parts, d_parts = ([w, core, far_a, far_b, both_a, both_b] for w, (far_a, core, both_a, far_b, both_b) in zip((w_g, w_u, w_d), got))
         bias_gu = [b.astype(F32)[None] for b in (bias_g, bias_u)]
-        inner = gate_up(idx, m, g_parts, u_parts, *bias_gu, TILE)
-        d_part = partial_rows(down_body, idx, inner, d_parts, (ch_count, SUB // 2, rows), TILE)
-        return finish_rows(ch_count, d_part, res, bias_d_r, m, *bias_gu, g_parts + u_parts + d_parts).reshape(tokens, local_width)
+        return finish_rows(ch_count, res, bias_d_r, m, *bias_gu, g_parts + u_parts + d_parts).reshape(tokens, local_width)
 
     return jax.shard_map(local_layer, mesh=mesh, in_specs=specs, out_specs=row_spec, check_vma=False)

time: 787 us -> 710 us (0.902)
  Pallas kernels: 582 us -> 521 us
  waiting for transfers between devices: 106 us -> 84.2 us
    pallas_call x1, Pallas kernels: 263 us -> 225 us  [residual_norm(): pl.pallas_call(functools.partial(line_body, 'norm', len(ship)), in_specs=...]
    ppermute x3, waiting for transfers between devices: 97.6 us -> 64.3 us  [local_layer(): lax.ppermute(vecs, 'wd', hop)]
    pallas_call x3 -> x1, Pallas kernels: 292 us -> 269 us  [finish_rows(): pl.pallas_call(functools.partial(line_body, 'finish', 0), in_specs=[VM, V...]
where the time goes in v2:
time: 710 us; the launch traced here: 709 us
  Pallas kernels  521 us (73%)
  waiting for transfers between devices  84.2 us (12%)
  matrix products  34.7 us (5%)
  local copies, waits for them, and re-layouts  24.9 us (4%)
  other arithmetic  17.6 us (2%)
  starting transfers between devices  13.4 us (2%)
  blocking collectives  12.7 us (2%)
    pallas_call x1, Pallas kernels, finish_rows(): pl.pallas_call(functools.partial(line_body, 'finish', 0), in_specs=[VM, V...  269 us
    pallas_call x1, Pallas kernels, residual_norm(): pl.pallas_call(functools.partial(line_body, 'norm', len(ship)), in_specs=...  225 us
    ppermute x3, waiting for transfers between devices, local_layer(): lax.ppermute(vecs, 'wd', hop)  64.3 us
    dot_general x6, matrix products, dot32(): return jnp.dot(a, b, preferred_element_type=F32)  34.7 us
    pallas_call x2, Pallas kernels, lru(): pl.pallas_call(lru_body, grid_spec=pltpu.PrefetchScalarGridSpec(num_scala...  27.6 us
  transfers between devices with their start and end apart: 18, of which 4 were waited for; matrix products, arithmetic and copies ran while one was open for 6% of the time, Pallas kernels for 4%

profile of v2, /device:TPU:0, one launch (start us, length us, event | category | flops | bytes accessed | tf_op | source)
XLA Modules:
  0.0 709.0 jit_solution(9957461565097695660)
XLA Ops:
  0.0 0.7 convert_add_fusion
  0.7 5.1 fusion
  5.8 12.7 %psum.7 = f32[4096,1]{0,1:T(1,128)S(1)} all-reduce(f32[4096,1]{0,1:T(1,128)S(1)} %bitcast.57), channel_id=1, replica_groups=mesh['dp'=2,'ch'=4,'wd'=4] {'wd'}, use_global_device_ids=true, to_apply=%region_1.2 | all-reduce | flops 4096 | bytes 32768 | tf_op jit(solution)/shard_map/psum | solution.py:580
  18.6 5.4 fusion.2
  24.0 1.9 constant_dynamic-slice_fusion.2
  25.9 1.8 copy-done
  27.7 8.6 %convolution_convert_fusion = bf16[3072,1024]{1,0:T(8,128)(2,1)} fusion(bf16[4096,1024]{1,0:T(8,128)(2,1)S(1)} %fusion.2, bf16[1024,256]{1,0:T(8,128)(2,1)S(1)} %get-tuple-element.60, bf16[1024,256]{1,0:T(8,128)(2,1)S(1)} %get-tuple-element.70, bf16[1024,256]{1,0:T(8,128)(2,1)S(1)} %get-tuple-element.58, bf16[1024,256]{1,0:T(8,128)(2,1)S(1)} %get-tuple-element.72), kind=kOutput, calls=%fused_computation.6 | convolution fusion | flops 6453985280 | bytes 14680064 | tf_op jit(solution)/shard_map/dot_general | solution.py:32
  37.0 2.3 constant_dynamic-slice_fusion
  39.3 1.6 collective-permute-start.14
  40.9 5.3 convolution_convert_fusion.1
  46.4 0.7 fusion.25
  47.1 8.5 %add_convert_fusion = bf16[3072,512]{1,0:T(8,128)(2,1)} fusion(bf16[3072,1024]{1,0:T(8,128)(2,1)} %collective-permute-done.8.peer_ref, bf16[1024,256]{1,0:T(8,128)(2,1)S(1)} %get-tuple-element.57, bf16[1024,256]{1,0:T(8,128)(2,1)S(1)} %get-tuple-element.73, bf16[4096,1024]{1,0:T(8,128)(2,1)} %copy-done), kind=kOutput, calls=%fused_computation.5 | convolution fusion | flops 3228041216 | bytes 13631488 | tf_op jit(solution)/shard_map/dot_general | solution.py:32
  56.0 0.7 maximum_maximum_fusion.conv_ref
  56.7 2.7 dynamic-slice_bitcast_fusion
  59.5 4.9 fusion.8.own_ref
  64.4 1.0 dynamic-slice_bitcast_fusion.3
  65.7 1.5 collective-permute-start.5
  67.1 0.6 pad_maximum_fusion.18
  68.0 64.3 %collective-permute-done.5 = bf16[3,1024]{1,0:T(4,128)(2,1)S(1)} collective-permute-done((bf16[3,1024]{1,0:T(4,128)(2,1)S(1)}, bf16[3,1024]{1,0:T(4,128)(2,1)S(1)}, u32[]{:S(2)}, u32[]{:S(2)}) %collective-permute-start.5) | collective-permute-done | bytes 6176 | tf_op jit(solution)/shard_map/ppermute | solution.py:567
  132.3 1.1 collective-permute-start.1
  133.4 1.5 collective-permute-start.15
  134.9 1.3 compare_select_fusion
  136.2 0.9 collective-permute-start.13
  137.1 3.5 add_convert_fusion.1
  140.6 2.9 collective-permute-done.2
  143.5 1.1 collective-permute-start.16
  144.6 10.3 %collective-permute-done.1 = bf16[256,1024]{1,0:T(8,128)(2,1)S(1)} collective-permute-done((bf16[256,1024]{1,0:T(8,128)(2,1)S(1)}, bf16[256,1024]{1,0:T(8,128)(2,1)S(1)}, u32[]{:S(2)}, u32[]{:S(2)}) %collective-permute-start.1) | collective-permute-done | bytes 524320 | tf_op jit(solution)/shard_map/ppermute | solution.py:576
  155.0 1.6 collective-permute-start.7
  156.6 0.6 pad_add_fusion.idx_ref
  157.2 1.7 copy.24.pos_ref
  158.9 0.7 pad_maximum_fusion.13.gate_w_ref
  159.6 4.0 fusion.16.own_ref
  163.6 0.5 collective-permute-start.17
  164.1 0.9 broadcast_1_tail_ref_carry_ref.2.tail_ref.carry_ref
  165.3 19.4 %lru.2 = (bf16[4,3,256,256]{3,2,1,0:T(8,128)(2,1)}, f32[8,256]{1,0:T(8,128)}, f32[8,256]{1,0:T(8,128)}) custom-call(s32[3]{0:T(128)} %pad_add_fusion.idx_ref, bf16[3072,512]{1,0:T(8,128)(2,1)} %fusion.8.own_ref, bf16[3072,1024]{1,0:T(8,128)(2,1)} %collective-permute-done.8.peer_ref, bf16[3072,512]{1,0:T(8,128)(2,1)} %copy-done.1, s32[3072,1]{1,0:T(8,128)} %copy.24.pos_ref, ...), custom_call_target="tpu_custom_call" | custom-call | flops 3145728000 | bytes 15728640 | tf_op jit(solution)/shard_map/lru/pallas_call | solution.py:101
  184.7 2.2 slice_bitcast_fusion
  186.9 0.9 collective-permute-start.12
  187.8 1.3 collective-permute-start.11
  189.1 0.6 broadcast_in_dim.30
  189.7 0.6 broadcast_in_dim.31
  190.3 1.0 copy.25.pos_ref
  191.4 0.7 fusion.24
  192.0 8.2 %lru.3 = (bf16[4,1,256,256]{3,2,1,0:T(8,128)(2,1)}, f32[8,256]{1,0:T(8,128)}, f32[8,256]{1,0:T(8,128)}) custom-call(s32[3]{0:T(128)} %pad_add_fusion.idx_ref, bf16[1024,512]{1,0:T(8,128)(2,1)} %fusion.16.own_ref, bf16[1024,1024]{1,0:T(8,128)(2,1)} %collective-permute-done.6.peer_ref, bf16[1024,512]{1,0:T(8,128)(2,1)} %collective-permute-done.7.far_ref, ...), custom_call_target="tpu_custom_call" | custom-call | flops 1048576000 | bytes 5242880 | tf_op jit(solution)/shard_map/lru/pallas_call | solution.py:101
  200.2 6.6 collective-permute-done.11.refs_9_
  206.8 0.7 copy-done.24
  207.7 224.8 %residual_norm.1 = (f32[16,4,16,1024]{3,2,1,0:T(8,128)}, bf16[4,16,16,4096]{3,2,1,0:T(8,128)(2,1)}, bf16[512,3072]{1,0:T(8,128)(2,1)}, bf16[1024,3072]{1,0:T(8,1...) custom-call(bf16[16,16,1024]{2,1,0:T(8,128)(2,1)} %bitcast.56, ...), custom_call_target="tpu_custom_call" | custom-call | flops 199999995904 | bytes 20000000 | tf_op jit(solution)/shard_map/residual_norm/pallas_call | solution.py:493
  432.5 268.8 %finish_rows.1 = (bf16[4,4,16,16,1024]{4,3,2,1,0:T(8,128)(2,1)}, bf16[768,1024]{1,0:T(8,128)(2,1)}, bf16[768,1024]{1,0:T(8,128)(2,1)}) custom-call(f32[16,4,16,1024]{3,2,1,0:T(8,128)} %get-tuple-element.31.refs_0_, f32[4,1,1024]{2,1,0:T(1,128)} %get-tuple-element.65.refs_1_, bf16[4,16,16,4096]{3,2,1,0:T(8,128)(2,1)} %get-tuple-element.32.refs_2_, ...), custom_call_target="tpu_custom_call" | custom-call | flops 199999995904 | bytes 20000000 | tf_op jit(solution)/shard_map/finish_rows/pallas_call | solution.py:517
  701.2 7.8 %copy.27 = bf16[4096,1024]{1,0:T(8,128)(2,1)} copy(bf16[4096,1024]{1,0:T(8,128)(2,1)} %bitcast.55) | data formatting | bytes 16777216
  (92 shorter events, 2.5 us)
Async XLA Ops:
  18.5 5.4 copy-start.2
  18.5 5.4 copy-start.3
  24.0 3.7 copy-start
  25.9 21.1 %copy-start.6 = (bf16[1024,256]{1,0:T(8,128)(2,1)}, bf16[1024,256]{1,0:T(8,128)(2,1)S(1)}, u32[]{:S(2)}) copy-start(bf16[1024,256]{1,0:T(8,128)(2,1)S(1)} %get-tuple-element.57) | copy-start | bytes 1572868
  25.9 21.2 %copy-start.8 = (bf16[1024,256]{1,0:T(8,128)(2,1)}, bf16[1024,256]{1,0:T(8,128)(2,1)S(1)}, u32[]{:S(2)}) copy-start(bf16[1024,256]{1,0:T(8,128)(2,1)S(1)} %get-tuple-element.73) | copy-start | bytes 1572868
  27.7 8.6 %copy-start.13 = (bf16[1024]{0:T(1024)(128)(2,1)S(1)}, bf16[1024]{0:T(1024)(128)(2,1)}, u32[]{:S(2)}) copy-start(bf16[1024]{0:T(1024)(128)(2,1)} %param.38) | copy-start | bytes 6148
  27.7 8.6 %copy-start.14 = (bf16[1024]{0:T(1024)(128)(2,1)S(1)}, bf16[1024]{0:T(1024)(128)(2,1)}, u32[]{:S(2)}) copy-start(bf16[1024]{0:T(1024)(128)(2,1)} %param.39) | copy-start | bytes 6148
  27.7 8.6 %copy-start.15 = (bf16[1024]{0:T(1024)(128)(2,1)S(1)}, bf16[1024]{0:T(1024)(128)(2,1)}, u32[]{:S(2)}) copy-start(bf16[1024]{0:T(1024)(128)(2,1)} %param.45) | copy-start | bytes 6148
  36.3 10.8 %collective-permute-start.8 = (bf16[3072,1024]{1,0:T(8,128)(2,1)}, bf16[3072,1024]{1,0:T(8,128)(2,1)}, u32[]{:S(2)}, u32[]{:S(2)}) collective-permute-start(bf16[3072,1024]{1,0:T(8,128)(2,1)} %convolution_convert_fusion), channel_id=1, source_target_pairs={{0,1},{1,0},{2,3},{3,2},{4,5},{5,4},{6,7},{7,6},{8,9},{9,8},{10,11... | collective-permute-start | bytes 18874376 | tf_op jit(solution)/shard_map/ppermute | solution.py:603
  36.4 29.3 %collective-permute-start.4 = (bf16[3,1024]{1,0:T(4,128)(2,1)S(1)}, bf16[3,1024]{1,0:T(4,128)(2,1)S(1)}, u32[]{:S(2)}, u32[]{:S(2)}) collective-permute-start(bf16[3,1024]{1,0:T(4,128)(2,1)S(1)} %pad_maximum_fusion.17), channel_id=1, source_target_pairs={{0,2},{1,3},{2,0},{3,1},{4,6},{5,7},{6,4},{7,5},{8,10},{9,11},{10,... | collective-permute-start | bytes 18440 | tf_op jit(solution)/shard_map/ppermute | solution.py:567
  36.8 30.9 %collective-permute-start.3 = (bf16[3,1024]{1,0:T(4,128)(2,1)S(1)}, bf16[3,1024]{1,0:T(4,128)(2,1)S(1)}, u32[]{:S(2)}, u32[]{:S(2)}) collective-permute-start(bf16[3,1024]{1,0:T(4,128)(2,1)S(1)} %pad_maximum_fusion.17), channel_id=1, source_target_pairs={{0,1},{1,0},{2,3},{3,2},{4,5},{5,4},{6,7},{7,6},{8,9},{9,8},{10,11... | collective-permute-start | bytes 18440 | tf_op jit(solution)/shard_map/ppermute | solution.py:567
  39.3 6.9 copy-start.16
  39.3 94.1 %collective-permute-start.14 = (bf16[512,1024]{1,0:T(8,128)(2,1)}, bf16[512,1024]{1,0:T(8,128)(2,1)}, u32[]{:S(2)}, u32[]{:S(2)}) collective-permute-start(bf16[512,1024]{1,0:T(8,128)(2,1)} %constant_dynamic-slice_fusion), channel_id=1, source_target_pairs={{0,2},{1,3},{2,0},{3,1},{4,6},{5,7},{6,4},{7,5},{8,10},{9,11},{10,... | collective-permute-start | bytes 3145736 | tf_op jit(solution)/shard_map/ppermute | solution.py:556
  46.2 90.0 %collective-permute-start.6 = (bf16[1024,1024]{1,0:T(8,128)(2,1)}, bf16[1024,1024]{1,0:T(8,128)(2,1)}, u32[]{:S(2)}, u32[]{:S(2)}) collective-permute-start(bf16[1024,1024]{1,0:T(8,128)(2,1)} %convolution_convert_fusion.1), channel_id=1, source_target_pairs={{0,1},{1,0},{2,3},{3,2},{4,5},{5,4},{6,7},{7,6},{8,9},{9,8},{10,11... | collective-permute-start | bytes 6291464 | tf_op jit(solution)/shard_map/ppermute | solution.py:603
  47.1 12.3 %slice-start = ((s8[8388608]{0:T(1024)(128)(4,1)}), s8[4194304]{0:T(1024)(128)(4,1)S(1)}, s32[]{:S(2)}) async-start(s8[8388608]{0:T(1024)(128)(4,1)} %bitcast.53), calls=%async_computation | async-start | bytes 8388608
  47.1 9.6 %copy-start.10 = (s32[1,4096]{1,0:T(1,128)S(1)}, s32[1,4096]{1,0:T(1,128)}, u32[]{:S(2)}) copy-start(s32[1,4096]{1,0:T(1,128)} %param.24) | copy-start | bytes 49156
  47.1 12.3 %slice-start.1 = ((s8[8388608]{0:T(1024)(128)(4,1)}), s8[4194304]{0:T(1024)(128)(4,1)S(1)}, s32[]{:S(2)}) async-start(s8[8388608]{0:T(1024)(128)(4,1)} %bitcast.53), calls=%async_computation.1 | async-start | bytes 8388608
  55.6 3.7 copy-start.4
  55.6 3.8 copy-start.5
  55.6 108.0 %collective-permute-start.9 = (bf16[3072,512]{1,0:T(8,128)(2,1)}, bf16[3072,512]{1,0:T(8,128)(2,1)S(1)}, u32[]{:S(2)}, u32[]{:S(2)}) collective-permute-start(bf16[3072,512]{1,0:T(8,128)(2,1)} %add_convert_fusion), channel_id=1, source_target_pairs={{0,2},{1,3},{2,0},{3,1},{4,6},{5,7},{6,4},{7,5},{8,10},{9,11},{10,... | collective-permute-start | bytes 9437192 | tf_op jit(solution)/shard_map/ppermute | solution.py:605
  59.4 6.0 copy-start.17
  59.4 6.0 copy-start.18
  59.4 6.1 copy-start.19
  59.4 6.2 copy-start.20
  59.4 77.7 %copy-start.7 = (bf16[1024,256]{1,0:T(8,128)(2,1)S(1)}, bf16[1024,256]{1,0:T(8,128)(2,1)}, u32[]{:S(2)}) copy-start(bf16[1024,256]{1,0:T(8,128)(2,1)} %copy-done.6) | copy-start | bytes 1572868
  59.4 77.7 %copy-start.9 = (bf16[1024,256]{1,0:T(8,128)(2,1)S(1)}, bf16[1024,256]{1,0:T(8,128)(2,1)}, u32[]{:S(2)}) copy-start(bf16[1024,256]{1,0:T(8,128)(2,1)} %copy-done.8) | copy-start | bytes 1572868
  65.7 66.6 %collective-permute-start.5 = (bf16[3,1024]{1,0:T(4,128)(2,1)S(1)}, bf16[3,1024]{1,0:T(4,128)(2,1)S(1)}, u32[]{:S(2)}, u32[]{:S(2)}) collective-permute-start(bf16[3,1024]{1,0:T(4,128)(2,1)S(1)} %pad_maximum_fusion.17), channel_id=1, source_target_pairs={{0,3},{1,2},{2,1},{3,0},{4,7},{5,6},{6,5},{7,4},{8,11},{9,10},{10,... | collective-permute-start | bytes 18440 | tf_op jit(solution)/shard_map/ppermute | solution.py:567
  67.7 75.8 %collective-permute-start.2 = (bf16[256,1024]{1,0:T(8,128)(2,1)S(1)}, bf16[256,1024]{1,0:T(8,128)(2,1)S(1)}, u32[]{:S(2)}, u32[]{:S(2)}) collective-permute-start(bf16[256,1024]{1,0:T(8,128)(2,1)S(1)} %get-tuple-element.49), channel_id=1, source_target_pairs={{0,3},{1,2},{2,1},{3,0},{4,7},{5,6},{6,5},{7,4},{8,11},{9,10},{10,... | collective-permute-start | bytes 1572872 | tf_op jit(solution)/shard_map/ppermute | solution.py:576
  132.3 22.7 %collective-permute-start.1 = (bf16[256,1024]{1,0:T(8,128)(2,1)S(1)}, bf16[256,1024]{1,0:T(8,128)(2,1)S(1)}, u32[]{:S(2)}, u32[]{:S(2)}) collective-permute-start(bf16[256,1024]{1,0:T(8,128)(2,1)S(1)} %get-tuple-element.50), channel_id=1, source_target_pairs={{0,2},{1,3},{2,0},{3,1},{4,6},{5,7},{6,4},{7,5},{8,10},{9,11},{10,... | collective-permute-start | bytes 1572872 | tf_op jit(solution)/shard_map/ppermute | solution.py:576
  133.4 30.2 %collective-permute-start.15 = (bf16[512,1024]{1,0:T(8,128)(2,1)}, bf16[512,1024]{1,0:T(8,128)(2,1)}, u32[]{:S(2)}, u32[]{:S(2)}) collective-permute-start(bf16[512,1024]{1,0:T(8,128)(2,1)} %collective-permute-done.14.refs_13_), channel_id=1, source_target_pairs={{0,16},{16,0},{1,17},{17,1},{2,18},{18,2},{3,19},{19,3},{4,20},{20... | collective-permute-start | bytes 3145736 | tf_op jit(solution)/shard_map/ppermute | solution.py:560
  136.2 64.0 %collective-permute-start.13 = (bf16[1024,1024]{1,0:T(8,128)(2,1)}, bf16[1024,1024]{1,0:T(8,128)(2,1)}, u32[]{:S(2)}, u32[]{:S(2)}) collective-permute-start(bf16[1024,1024]{1,0:T(8,128)(2,1)} %refs_11_.2), channel_id=1, source_target_pairs={{0,1},{1,0},{2,3},{3,2},{4,5},{5,4},{6,7},{7,6},{8,9},{9,8},{10,11... | collective-permute-start | bytes 6291464 | tf_op jit(solution)/shard_map/ppermute | solution.py:561
  143.5 11.4 %copy-start.21 = (bf16[256,1024]{1,0:T(8,128)(2,1)}, bf16[256,1024]{1,0:T(8,128)(2,1)S(1)}, u32[]{:S(2)}) copy-start(bf16[256,1024]{1,0:T(8,128)(2,1)S(1)} %collective-permute-done.2) | copy-start | bytes 1572868
  143.5 44.3 %collective-permute-start.16 = (bf16[512,1024]{1,0:T(8,128)(2,1)}, bf16[512,1024]{1,0:T(8,128)(2,1)}, u32[]{:S(2)}, u32[]{:S(2)}) collective-permute-start(bf16[512,1024]{1,0:T(8,128)(2,1)} %collective-permute-done.14.refs_13_), channel_id=1, source_target_pairs={{0,1},{1,0},{2,3},{3,2},{4,5},{5,4},{6,7},{7,6},{8,9},{9,8},{10,11... | collective-permute-start | bytes 3145736 | tf_op jit(solution)/shard_map/ppermute | solution.py:562
  155.0 1.6 copy-start.22
  155.0 34.1 %collective-permute-start.7 = (bf16[1024,512]{1,0:T(8,128)(2,1)}, bf16[1024,512]{1,0:T(8,128)(2,1)}, u32[]{:S(2)}, u32[]{:S(2)}) collective-permute-start(bf16[1024,512]{1,0:T(8,128)(2,1)} %add_convert_fusion.1), channel_id=1, source_target_pairs={{0,2},{1,3},{2,0},{3,1},{4,6},{5,7},{6,4},{7,5},{8,10},{9,11},{10,... | collective-permute-start | bytes 3145736 | tf_op jit(solution)/shard_map/ppermute | solution.py:605
  163.6 23.3 %collective-permute-start = (bf16[256,1024]{1,0:T(8,128)(2,1)}, bf16[256,1024]{1,0:T(8,128)(2,1)}, u32[]{:S(2)}, u32[]{:S(2)}) collective-permute-start(bf16[256,1024]{1,0:T(8,128)(2,1)} %get-tuple-element.51), channel_id=1, source_target_pairs={{0,1},{1,0},{2,3},{3,2},{4,5},{5,4},{6,7},{7,6},{8,9},{9,8},{10,11... | collective-permute-start | bytes 1572872 | tf_op jit(solution)/shard_map/ppermute | solution.py:576
  163.6 1.7 copy-start.1
  163.6 36.5 %collective-permute-start.17 = (bf16[512,1024]{1,0:T(8,128)(2,1)}, bf16[512,1024]{1,0:T(8,128)(2,1)}, u32[]{:S(2)}, u32[]{:S(2)}) collective-permute-start(bf16[512,1024]{1,0:T(8,128)(2,1)} %collective-permute-done.15.refs_14_), channel_id=1, source_target_pairs={{0,1},{1,0},{2,3},{3,2},{4,5},{5,4},{6,7},{7,6},{8,9},{9,8},{10,11... | collective-permute-start | bytes 3145736 | tf_op jit(solution)/shard_map/ppermute | solution.py:563
  184.7 4.4 copy-start.11
  184.7 5.0 copy-start.12
  186.9 13.3 %collective-permute-start.12 = (bf16[3,256,256]{2,1,0:T(8,128)(2,1)S(1)}, bf16[3,256,256]{2,1,0:T(8,128)(2,1)S(1)}, u32[]{:S(2)}, u32[]{:S(2)}) collective-permute-start(bf16[3,256,256]{2,1,0:T(8,128)(2,1)S(1)} %get-tuple-element.61), channel_id=1, source_target_pairs={{0,3},{1,2},{2,1},{3,0},{4,7},{5,6},{6,5},{7,4},{8,11},{9,10},{10,... | collective-permute-start | bytes 1179656 | tf_op jit(solution)/shard_map/ppermute | solution.py:609
  187.8 19.0 %collective-permute-start.11 = (bf16[3,256,256]{2,1,0:T(8,128)(2,1)S(1)}, bf16[3,256,256]{2,1,0:T(8,128)(2,1)S(1)}, u32[]{:S(2)}, u32[]{:S(2)}) collective-permute-start(bf16[3,256,256]{2,1,0:T(8,128)(2,1)S(1)} %get-tuple-element.62), channel_id=1, source_target_pairs={{0,2},{1,3},{2,0},{3,1},{4,6},{5,7},{6,4},{7,5},{8,10},{9,11},{10,... | collective-permute-start | bytes 1179656 | tf_op jit(solution)/shard_map/ppermute | solution.py:609
  189.1 17.7 %collective-permute-start.10 = (bf16[3,256,256]{2,1,0:T(8,128)(2,1)S(1)}, bf16[3,256,256]{2,1,0:T(8,128)(2,1)S(1)}, u32[]{:S(2)}, u32[]{:S(2)}) collective-permute-start(bf16[3,256,256]{2,1,0:T(8,128)(2,1)S(1)} %get-tuple-element.63), channel_id=1, source_target_pairs={{0,1},{1,0},{2,3},{3,2},{4,5},{5,4},{6,7},{7,6},{8,9},{9,8},{10,11... | collective-permute-start | bytes 1179656 | tf_op jit(solution)/shard_map/ppermute | solution.py:609
  200.2 6.6 copy-start.23
  206.8 0.8 copy-start.24
  206.8 0.9 copy-start.25

commit v3 on v2

--- a/solution.py
+++ b/solution.py
@@ -116,15 +116,15 @@
 
 def line_body(kind, n_ship, *refs):
     if kind == "norm":
-        x_rows, (bias, gain, mixed), mix_in, o_parts = refs[:4], refs[4:7], refs[7:11], refs[11:17]
-        ship, refs = refs[17:17 + n_ship], refs[17 + n_ship:]
+        (bias, gain, x_line, mixed), mix_in, o_parts = refs[:4], refs[4:8], refs[8:14]
+        ship, refs = refs[14:14 + n_ship], refs[14 + n_ship:]
         res_ref, out = refs[:2]
         shipped, refs = refs[2:2 + 5 * n_ship], refs[2 + 5 * n_ship:]
-        rbuf, obuf, send, recv, loc, w_send, w_recv, part, mixbuf, wo, a_send, a_recv, pre_sem = refs
+        rbuf, obuf, send, recv, loc, w_send, w_recv, part, mixbuf, wo, a_send, a_recv, pre_sem, xbuf, x_send, x_recv = refs
     else:
         res_ref, bias, m_all, bias_g, bias_u = refs[:5]
         g_parts, u_parts, d_parts = refs[5:11], refs[11:17], refs[17:23]
-        out, late_b, late_both, rbuf, obuf, send, recv, loc, a_send, a_recv, part, mbuf, inner, wbuf, pre_sem, tile_sem, l_send, l_recv = refs[23:]
+        out, late_b, late_both, late_a, late_both_a, rbuf, obuf, send, recv, loc, a_send, a_recv, part, mbuf, inner, wbuf, pre_sem, tile_sem, l_send, l_recv = refs[23:]
     n = rbuf.shape[1] + 1
     steps = rbuf.shape[2]
     z, me, dp = lax.axis_index('ch'), lax.axis_index('wd'), lax.axis_index('dp')
@@ -187,7 +187,7 @@
     def weight_copy(q, j):
         i, p = q // PIECES, q % PIECES
         far_a, core, both_a, far_b, both_b = shipped[5 * i:5 * i + 5]
-        size = far_a.shape[0] // PIECES
+        size = ship[i].shape[0] // (2 * PIECES)
         own_at, at = pl.ds((PIECES * dp + p) * size, size), pl.ds(p * size, size)
         if j == 4:
             src, dst = ship[i], core
@@ -208,16 +208,21 @@
         there_at = mixbuf.at[me ^ r if landed else me, pl.ds(n - mixed.shape[1], mixed.shape[1])]
         return pltpu.make_async_remote_copy(src_ref=mixed.at[r], dst_ref=there_at, send_sem=a_send.at[r - 1], recv_sem=a_recv.at[r - 1], device_id=wd_to(r), device_id_type=MESH)
 
+    def row_copy(r):
+        return pltpu.make_async_remote_copy(src_ref=x_line.at[me ^ r], dst_ref=xbuf.at[r], send_sem=x_send.at[r - 1], recv_sem=x_recv.at[r - 1], device_id=wd_to(r), device_id_type=MESH)
+
     if kind == "norm":
         for r in OTHERS:
             mix_copy(r, False).start()
-        jobs = [(mixed.at[0], mixbuf.at[me, pl.ds(n - mixed.shape[1], mixed.shape[1])])]
+        for r in OTHERS:
+            row_copy(r).start()
+        jobs = [(x_line.at[me], xbuf.at[0]), (mixed.at[0], mixbuf.at[me, pl.ds(n - mixed.shape[1], mixed.shape[1])])]
         jobs += [(src, mixbuf.at[me ^ r, pl.ds(0, src.shape[0])]) for r, src in enumerate(mix_in)]
         jobs += [(w, wo.at[pl.ds(to, w.shape[0])]) for w, to in row_places(o_parts)]
         loads = [pltpu.make_async_copy(src, dst, pre_sem.at[j]) for j, (src, dst) in enumerate(jobs)]
         for copy in loads:
             copy.start()
-        for q in range(PIECES * n_ship):
+        for q in range(PIECES * n_ship - 1):
             weight_copy(q, 0).start()
         for i in range(n_ship):
             weight_copy(PIECES * i, 4).start()
@@ -257,10 +262,10 @@
             else:
                 at = pl.ds(pl.multiple_of(lax.rem(q - gates, per_block) * TILE, TILE), TILE)
                 own, core, far_a, far_b, both_a, both_b = d_parts
-                rows_a = dp * far_a.shape[0]
-                rows_b = far_a.shape[0] - rows_a
-                late = rows_b + far_b.shape[0]
-                jobs = ([(own, 0, 0)], [(core, 0, 0)], [(far_a, 0, rows_a), (far_b, 0, rows_b), (late_b, 0, late)], [(both_a, 0, rows_a), (both_b, 0, rows_b), (late_both, 0, late)])[down_block]
+                rows_a = dp * (own.shape[0] // 2)
+                rows_b = own.shape[0] // 2 - rows_a
+                late, late_y = rows_b + far_b.shape[0], rows_a + far_a.shape[0]
+                jobs = ([(own, 0, 0)], [(core, 0, 0)], [(far_a, 0, rows_a), (far_b, 0, rows_b), (late_b, 0, late), (late_a, 0, late_y)], [(both_a, 0, rows_a), (both_b, 0, rows_b), (late_both, 0, late), (late_both_a, 0, late_y)])[down_block]
             return [pltpu.make_async_copy(w.at[:, at], wbuf.at[slot, i, pl.ds(to, w.shape[0]), :], tile_sem.at[slot, j]) for j, (w, i, to) in enumerate(jobs)]
 
         def for_tile(q, act):
@@ -276,23 +281,42 @@
                         act(copy)
 
         def late_copy(j):
-            far_a, size = d_parts[2], late_b.shape[0]
-            src, dst, to = ((far_a.at[pl.ds(size, size)], late_b, {'dp': 1 - dp}), (late_b, late_both, wd_to(1)))[j]
+            size = late_a.shape[0]
+            own, far_a = d_parts[0], d_parts[2]
+            one, two = pl.ds(0, size), pl.ds(size, size)
+            src, dst, to = (
+                (far_a.at[pl.ds(far_a.shape[0] - size, size)], late_b.at[one], {'dp': 1 - dp}),
+                (own.at[pl.ds((PIECES * dp + PIECES - 1) * size, size)], late_a, wd_to(2)),
+                (late_a, late_b.at[two], {'dp': 1 - dp}),
+                (late_a, late_both_a, wd_to(1)),
+                (late_b.at[one], late_both.at[one], wd_to(1)),
+                (late_b.at[two], late_both.at[two], wd_to(1)),
+            )[j]
             return pltpu.make_async_remote_copy(src_ref=src, dst_ref=dst, send_sem=l_send.at[j], recv_sem=l_recv.at[j], device_id=to, device_id_type=MESH)
 
         late_copy(0).start()
+        late_copy(1).start()
 
         def mlp_tile(job, _):
             phase, q = lax.div(job, tiles), lax.rem(job, tiles)
 
+            @pl.when(job == gates // 2)
+            def _():
+                late_copy(1).wait_recv()
+                late_copy(2).start()
+                late_copy(3).start()
+
             @pl.when(job == gates + per_block)
             def _():
                 late_copy(0).wait_recv()
-                late_copy(1).start()
+                late_copy(4).start()
+                late_copy(2).wait_recv()
+                late_copy(5).start()
 
             @pl.when(job == gates + 3 * per_block - 1)
             def _():
-                late_copy(1).wait_recv()
+                for j in OTHERS:
+                    late_copy(j + 2).wait_recv()
 
             for_tile(q, lambda copy: copy.wait())
 
@@ -342,7 +366,7 @@
             val = val + jnp.where(z > 0, rbuf[0, n - 2, s, r].astype(F32), 0.0)
             val = val + jnp.where(z < n - 1, rbuf[1, n - 2, s, r].astype(F32), 0.0)
             if kind == "norm":
-                val = x_rows[r][s].astype(F32) + val + bias[r]
+                val = xbuf[r, s].astype(F32) + val + bias[r]
                 res_ref[s, r] = val
                 total = total + jnp.sum(val * val, axis=1, keepdims=True)
             else:
@@ -359,6 +383,12 @@
         local_copy(s).start()
 
     def step(t, _):
+        if kind == "norm":
+            @pl.when(t == n - 1)
+            def _():
+                for r in OTHERS:
+                    row_copy(r).wait_recv()
+
         for h in range(n, 0, -1):
             s = t - (n - 1) - lag - (h - 1)
 
@@ -414,8 +444,8 @@
                 lax.fori_loop(tiles + lax.div(t * tiles, half), tiles + lax.div((t + 1) * tiles, half), mlp_tile, 0)
 
         if kind == "norm":
-            for q in range(PIECES * n_ship):
-                @pl.when(t == (3 * q + 5) // 2)
+            for q in range(PIECES * n_ship - 1):
+                @pl.when(t == (3 * q + 8) // 2)
                 def _(q=q):
                     weight_copy(q, 0).wait_recv()
                     if q < crossed:
@@ -423,7 +453,7 @@
                     weight_copy(q, 2).start()
 
                 if q < crossed:
-                    @pl.when(t == (3 * q + 10) // 2)
+                    @pl.when(t == (3 * q + 12) // 2)
                     def _(q=q):
                         weight_copy(q, 1).wait_recv()
                         weight_copy(q, 3).start()
@@ -450,12 +480,12 @@
         return 0
 
     if kind != "norm":
-        for j in WAYS:
+        for j in range(6):
             late_copy(j).wait_send()
 
     lax.fori_loop(0, steps, drain, 0)
     if kind == "norm":
-        for q in range(PIECES * n_ship):
+        for q in range(PIECES * n_ship - 1):
             weight_copy(q, 0).wait_send()
             weight_copy(q, 2).wait()
             if q < crossed:
@@ -465,6 +495,7 @@
             weight_copy(PIECES * i, 4).wait()
         for r in OTHERS:
             mix_copy(r, False).wait_send()
+            row_copy(r).wait_send()
 
 
 VM = pl.BlockSpec(memory_space=pltpu.VMEM)
@@ -477,22 +508,19 @@
     return [pltpu.VMEM((2, n - 1, steps) + block, BF16), pltpu.VMEM((steps,) + done, BF16), DMA(sems), DMA(sems), DMA((steps,))]
 
 
-def residual_norm(n, xs, bias, gain, mixed, mix_in, o_parts, ship):
-    steps, rows, width = xs[0].shape
+def residual_norm(n, x_line, bias, gain, mixed, mix_in, o_parts, ship):
+    _, steps, rows, width = x_line.shape
     out_w = []
     for w in ship:
-        half = jax.ShapeDtypeStruct((w.shape[0] // 2, w.shape[1]), BF16)
-        if w is ship[-1]:
-            late = jax.ShapeDtypeStruct((w.shape[0] // 4, w.shape[1]), BF16)
-        else:
-            late = half
-        out_w += [half, jax.ShapeDtypeStruct(w.shape, BF16), half, late, late]
+        less = 1 if w is ship[-1] else 0
+        near, late = (jax.ShapeDtypeStruct((w.shape[0] // (2 * PIECES) * (PIECES - k), w.shape[1]), BF16) for k in (less, 2 * less))
+        out_w += [near, jax.ShapeDtypeStruct(w.shape, BF16), near, late, late]
     done = (rows, 4 * width)
-    far = [mixed, *mix_in, *o_parts, *ship]
+    far = [x_line, mixed, *mix_in, *o_parts, *ship]
     pieces = PIECES * len(ship)
     outs = pl.pallas_call(
         functools.partial(line_body, "norm", len(ship)),
-        in_specs=[VM] * 6 + [ANY] * len(far),
+        in_specs=[VM] * 2 + [ANY] * len(far),
         out_specs=[VM, ANY] + [ANY] * len(out_w),
         out_shape=[jax.ShapeDtypeStruct((steps, 4, rows, width), F32), jax.ShapeDtypeStruct((n, steps) + done, BF16)] + out_w,
         scratch_shapes=line_scratch(n, steps, (4, rows, width), done) + [
@@ -500,32 +528,34 @@
             pltpu.VMEM((n, steps, 4, rows, width), BF16),
             pltpu.VMEM((4, n) + mixed.shape[2:], BF16),
             pltpu.VMEM((4 * width, width), BF16),
-            DMA((3,)), DMA((3,)), DMA((11,)),
+            DMA((3,)), DMA((3,)), DMA((12,)),
+            pltpu.VMEM(x_line.shape, BF16), DMA((3,)), DMA((3,)),
         ],
         compiler_params=pltpu.CompilerParams(collective_id=0, has_side_effects=True, vmem_limit_bytes=LIMIT),
         cost_estimate=WORK,
         name="residual_norm",
-    )(*xs, bias, gain, *far)
+    )(bias, gain, *far)
     return outs[0], outs[1], [outs[2 + 5 * i:7 + 5 * i] for i in range(len(ship))]
 
 
 def finish_rows(n, res, bias, m_all, bias_g, bias_u, pieces):
     steps, _, rows, width = res.shape
     half = steps // 2
+    late = pieces[-1].shape[0] // 2
     inner_width = bias_g.shape[1]
     toks = n * half * rows
     return pl.pallas_call(
         functools.partial(line_body, "finish", 0),
         in_specs=[VM, VM, ANY, VM, VM] + [ANY] * len(pieces),
-        out_specs=[ANY] * 3,
-        out_shape=[jax.ShapeDtypeStruct((n, 4, steps, rows, width), BF16)] + [jax.ShapeDtypeStruct(pieces[-1].shape, BF16)] * 2,
+        out_specs=[ANY] * 5,
+        out_shape=[jax.ShapeDtypeStruct((n, 4, steps, rows, width), BF16)] + [jax.ShapeDtypeStruct((late * k, pieces[-1].shape[1]), BF16) for k in (2, 2, 1, 1)],
         scratch_shapes=line_scratch(n, steps, (4, rows, width), (4, rows, width)) + [
             DMA((3, steps)), DMA((3, steps)),
             pltpu.VMEM((n, steps, 4, rows, width), BF16),
             pltpu.VMEM((2, n, half) + m_all.shape[2:], BF16),
             pltpu.VMEM((toks, inner_width), BF16),
             pltpu.VMEM((2, 2, 4 * width, TILE), BF16),
-            DMA((2,)), DMA((2, 12)), DMA((2,)), DMA((2,)),
+            DMA((2,)), DMA((2, 12)), DMA((6,)), DMA((6,)),
         ],
         compiler_params=pltpu.CompilerParams(collective_id=1, has_side_effects=True, vmem_limit_bytes=LIMIT),
         cost_estimate=WORK,
@@ -570,11 +600,7 @@
 
         blocks = resid_in.reshape(ch_count, wd_count, share, local_width)
         line = lax.dynamic_index_in_dim(blocks, z, 0, keepdims=False)
-        x_rows = [lax.dynamic_index_in_dim(line, me ^ r, 0, keepdims=False) for r in range(4)]
-        early = []
-        for r, hop in zip(OTHERS, (core_hop, y_hop, both_hop)):
-            early.append(lax.ppermute(x_rows[r], 'wd', hop))
-        x_rows = [x_rows[0]] + early
+        line = line.reshape(wd_count, SUB, rows, local_width)
 
         resid32 = resid_in.astype(F32)
         sum_sq = lax.psum(jnp.sum(resid32 * resid32, axis=1, keepdims=True), 'wd')
@@ -607,8 +633,7 @@
             mixed, tail, carry = lru(idx, own, sent, far, pos[start:stop], bias_xy, conv, soft, gate_w, gate_b, tail, carry, share)
             if k == 0:
                 mix_in = [mixed[0]] + [lax.ppermute(mixed[r], 'wd', hop) for r, hop in zip(OTHERS, (core_hop, y_hop, both_hop))]
-        x_rows = [x.reshape(SUB, rows, local_width) for x in x_rows]
-        res, m, got = residual_norm(ch_count, x_rows, bias_o_r, gain_r, mixed, mix_in, w_o_parts, [w_g, w_u, w_d])
+        res, m, got = residual_norm(ch_count, line, bias_o_r, gain_r, mixed, mix_in, w_o_parts, [w_g, w_u, w_d])
         g_parts, u_parts, d_parts = ([w, core, far_a, far_b, both_a, both_b] for w, (far_a, core, both_a, far_b, both_b) in zip((w_g, w_u, w_d), got))
         bias_gu = [b.astype(F32)[None] for b in (bias_g, bias_u)]
         return finish_rows(ch_count, res, bias_d_r, m, *bias_gu, g_parts + u_parts + d_parts).reshape(tokens, local_width)

time: 710 us -> 692 us (0.975)
  waiting for transfers between devices: 84.2 us -> 56.6 us
  Pallas kernels: 521 us -> 533 us
    ppermute x3, waiting for transfers between devices: 64.3 us -> 0.2 us  [local_layer(): lax.ppermute(vecs, 'wd', hop)]
    ppermute x2, waiting for transfers between devices: 0.01 us -> 43.2 us  [local_layer(): far = lax.ppermute(far, 'wd', y_hop)]
    ppermute x3 -> x0, waiting for transfers between devices: 13.3 us -> none  [local_layer(): early.append(lax.ppermute(x_rows[r], 'wd', hop))]
    pallas_call x1, Pallas kernels: 225 us -> 234 us  [residual_norm(): pl.pallas_call(functools.partial(line_body, 'norm', len(ship)), in_specs=...]
    ppermute x1, waiting for transfers between devices: 0.01 us -> 8.17 us  [gathered(): far_b = lax.ppermute(far_a, 'dp', flip_pairs(2, 1))]
  transfers between devices with their start and end apart: 18 -> 15, of which waited for: 4 -> 5; matrix products, arithmetic and copies ran while one was open for 6% -> 7% of each run, Pallas kernels for 4% -> 4%
where the time goes in v3:
time: 692 us; the launch traced here: 691 us
  Pallas kernels  533 us (77%)
  waiting for transfers between devices  56.6 us (8%)
  matrix products  35.7 us (5%)
  local copies, waits for them, and re-layouts  26 us (4%)
  other arithmetic  17.7 us (3%)
  blocking collectives  12.7 us (2%)
  starting transfers between devices  9.16 us (1%)
    pallas_call x1, Pallas kernels, finish_rows(): pl.pallas_call(functools.partial(line_body, 'finish', 0), in_specs=[VM, V...  271 us
    pallas_call x1, Pallas kernels, residual_norm(): pl.pallas_call(functools.partial(line_body, 'norm', len(ship)), in_specs=...  234 us
    ppermute x2, waiting for transfers between devices, local_layer(): far = lax.ppermute(far, 'wd', y_hop)  43.2 us
    dot_general x6, matrix products, dot32(): return jnp.dot(a, b, preferred_element_type=F32)  35.7 us
    pallas_call x2, Pallas kernels, lru(): pl.pallas_call(lru_body, grid_spec=pltpu.PrefetchScalarGridSpec(num_scala...  27.7 us
  transfers between devices with their start and end apart: 15, of which 5 were waited for; matrix products, arithmetic and copies ran while one was open for 7% of the time, Pallas kernels for 4%

profile of v3, /device:TPU:0, one launch (start us, length us, event | category | flops | bytes accessed | tf_op | source)
XLA Modules:
  0.0 690.9 jit_solution(11343433671608027299)
XLA Ops:
  0.0 0.7 convert_add_fusion
  0.7 5.1 fusion
  5.8 12.7 %psum.7 = f32[4096,1]{0,1:T(1,128)S(1)} all-reduce(f32[4096,1]{0,1:T(1,128)S(1)} %bitcast.48), channel_id=1, replica_groups=mesh['dp'=2,'ch'=4,'wd'=4] {'wd'}, use_global_device_ids=true, to_apply=%region_1.2 | all-reduce | flops 4096 | bytes 32768 | tf_op jit(solution)/shard_map/psum | solution.py:606
  18.6 5.4 fusion.2
  24.0 1.9 constant_dynamic-slice_fusion.2
  25.9 1.8 copy-done
  27.7 8.6 %convolution_convert_fusion = bf16[3072,1024]{1,0:T(8,128)(2,1)} fusion(bf16[4096,1024]{1,0:T(8,128)(2,1)S(1)} %fusion.2, bf16[1024,256]{1,0:T(8,128)(2,1)S(1)} %get-tuple-element.56, bf16[1024,256]{1,0:T(8,128)(2,1)S(1)} %get-tuple-element.64, bf16[1024,256]{1,0:T(8,128)(2,1)S(1)} %get-tuple-element.54, bf16[1024,256]{1,0:T(8,128)(2,1)S(1)} %get-tuple-element.66), kind=kOutput, calls=%fused_computation.6 | convolution fusion | flops 6453985280 | bytes 14680064 | tf_op jit(solution)/shard_map/dot_general | solution.py:32
  36.4 0.5 collective-permute-start.1
  36.8 0.2 collective-permute-start.10
  37.1 2.3 constant_dynamic-slice_fusion
  39.3 1.7 collective-permute-start.11
  41.0 5.3 convolution_convert_fusion.1
  46.6 0.7 fusion.25
  47.3 1.1 dynamic-slice_bitcast_fusion
  48.5 8.5 %add_convert_fusion = bf16[3072,512]{1,0:T(8,128)(2,1)} fusion(bf16[3072,1024]{1,0:T(8,128)(2,1)} %collective-permute-done.5.peer_ref, bf16[1024,256]{1,0:T(8,128)(2,1)S(1)} %get-tuple-element.53, bf16[1024,256]{1,0:T(8,128)(2,1)S(1)} %get-tuple-element.67, bf16[4096,1024]{1,0:T(8,128)(2,1)} %copy-done), kind=kOutput, calls=%fused_computation.5 | convolution fusion | flops 3228041216 | bytes 13631488 | tf_op jit(solution)/shard_map/dot_general | solution.py:32
  57.0 0.4 collective-permute-start.6
  57.4 0.6 pad_maximum_fusion.18
  58.2 0.7 maximum_maximum_fusion.conv_ref
  58.9 4.9 fusion.8.own_ref
  63.8 2.0 collective-permute-done.11.refs_10_
  65.7 1.6 collective-permute-start.12
  67.3 1.4 compare_select_fusion
  68.7 4.4 add_convert_fusion.1
  73.1 1.5 collective-permute-start.4
  74.6 0.6 pad_add_fusion.idx_ref
  75.2 1.7 copy.24.pos_ref
  76.9 0.7 pad_maximum_fusion.13.gate_w_ref
  77.6 4.1 fusion.16.own_ref
  81.7 8.2 %collective-permute-done.12.refs_11_ = bf16[512,1024]{1,0:T(8,128)(2,1)} collective-permute-done((bf16[512,1024]{1,0:T(8,128)(2,1)}, bf16[512,1024]{1,0:T(8,128)(2,1)}, u32[]{:S(2)}, u32[]{:S(2)}) %collective-permute-start.12) | collective-permute-done | bytes 1048608 | tf_op jit(solution)/shard_map/ppermute | solution.py:590
  89.9 43.2 %collective-permute-done.6.far_ref = bf16[3072,512]{1,0:T(8,128)(2,1)S(1)} collective-permute-done((bf16[3072,512]{1,0:T(8,128)(2,1)}, bf16[3072,512]{1,0:T(8,128)(2,1)S(1)}, u32[]{:S(2)}, u32[]{:S(2)}) %collective-permute-start.6) | collective-permute-done | bytes 3145760 | tf_op jit(solution)/shard_map/ppermute | solution.py:631
  133.1 0.6 broadcast_1_tail_ref_carry_ref.2.tail_ref.carry_ref
  133.7 1.0 copy-done.1
  134.7 19.5 %lru.2 = (bf16[4,3,256,256]{3,2,1,0:T(8,128)(2,1)}, f32[8,256]{1,0:T(8,128)}, f32[8,256]{1,0:T(8,128)}) custom-call(s32[3]{0:T(128)} %pad_add_fusion.idx_ref, bf16[3072,512]{1,0:T(8,128)(2,1)} %fusion.8.own_ref, bf16[3072,1024]{1,0:T(8,128)(2,1)} %collective-permute-done.5.peer_ref, bf16[3072,512]{1,0:T(8,128)(2,1)} %copy-done.1, s32[3072,1]{1,0:T(8,128)} %copy.24.pos_ref, ...), custom_call_target="tpu_custom_call" | custom-call | flops 3145728000 | bytes 15728640 | tf_op jit(solution)/shard_map/lru/pallas_call | solution.py:101
  154.3 0.7 collective-permute-start.2
  155.0 2.2 slice_bitcast_fusion
  157.4 0.9 collective-permute-start.9
  158.3 1.6 collective-permute-start.8
  160.0 0.6 broadcast_in_dim.30
  160.6 0.6 broadcast_in_dim.31
  161.2 1.0 copy.25.pos_ref
  162.2 3.1 constant_dynamic-slice_fusion.10
  165.3 0.7 fusion.24
  165.9 8.2 %lru.3 = (bf16[4,1,256,256]{3,2,1,0:T(8,128)(2,1)}, f32[8,256]{1,0:T(8,128)}, f32[8,256]{1,0:T(8,128)}) custom-call(s32[3]{0:T(128)} %pad_add_fusion.idx_ref, bf16[1024,512]{1,0:T(8,128)(2,1)} %fusion.16.own_ref, bf16[1024,1024]{1,0:T(8,128)(2,1)} %collective-permute-done.3.peer_ref, bf16[1024,512]{1,0:T(8,128)(2,1)} %collective-permute-done.4.far_ref, ...), custom_call_target="tpu_custom_call" | custom-call | flops 1048576000 | bytes 5242880 | tf_op jit(solution)/shard_map/lru/pallas_call | solution.py:101
  174.1 3.1 collective-permute-done.8.refs_6_
  177.3 0.7 copy-done.20
  178.2 234.1 %residual_norm.1 = (f32[16,4,16,1024]{3,2,1,0:T(8,128)}, bf16[4,16,16,4096]{3,2,1,0:T(8,128)(2,1)}, bf16[512,3072]{1,0:T(8,128)(2,1)}, bf16[1024,3072]{1,0:T(8,1...) custom-call(f32[4,1,1024]{2,1,0:T(1,128)} %get-tuple-element.63.refs, ...), custom_call_target="tpu_custom_call" | custom-call | flops 199999995904 | bytes 20000000 | tf_op jit(solution)/shard_map/residual_norm/pallas_call | solution.py:521
  412.3 270.8 %finish_rows.1 = (bf16[4,4,16,16,1024]{4,3,2,1,0:T(8,128)(2,1)}, bf16[768,1024]{1,0:T(8,128)(2,1)}, bf16[768,1024]{1,0:T(8,128)(2,1)}, bf16[384,1024]{1,0:T(8,128)(2,1)}, bf16[384,1024]{1,0:T(8,128)(2,1)}) custom-call(f32[16,4,16,1024]{3,2,1,0:T(8,128)} %get-tuple-element.31.refs_0_, f32[4,1,1024]{2,1,0:T(1,128)} %get-tuple-element.61.refs_1_, ...), custom_call_target="tpu_custom_call" | custom-call | flops 199999995904 | bytes 20000000 | tf_op jit(solution)/shard_map/finish_rows/pallas_call | solution.py:547
  683.1 7.8 %copy.27 = bf16[4096,1024]{1,0:T(8,128)(2,1)} copy(bf16[4096,1024]{1,0:T(8,128)(2,1)} %bitcast.46) | data formatting | bytes 16777216
  (78 shorter events, 1.0 us)
Async XLA Ops:
  18.5 5.4 copy-start.2
  18.5 5.4 copy-start.3
  24.0 3.7 copy-start
  25.9 22.5 %copy-start.6 = (bf16[1024,256]{1,0:T(8,128)(2,1)}, bf16[1024,256]{1,0:T(8,128)(2,1)S(1)}, u32[]{:S(2)}) copy-start(bf16[1024,256]{1,0:T(8,128)(2,1)S(1)} %get-tuple-element.53) | copy-start | bytes 1572868
  25.9 22.5 %copy-start.7 = (bf16[1024,256]{1,0:T(8,128)(2,1)}, bf16[1024,256]{1,0:T(8,128)(2,1)S(1)}, u32[]{:S(2)}) copy-start(bf16[1024,256]{1,0:T(8,128)(2,1)S(1)} %get-tuple-element.67) | copy-start | bytes 1572868
  27.7 8.6 %copy-start.11 = (bf16[1024]{0:T(1024)(128)(2,1)S(1)}, bf16[1024]{0:T(1024)(128)(2,1)}, u32[]{:S(2)}) copy-start(bf16[1024]{0:T(1024)(128)(2,1)} %param.38) | copy-start | bytes 6148
  27.7 8.6 %copy-start.12 = (bf16[1024]{0:T(1024)(128)(2,1)S(1)}, bf16[1024]{0:T(1024)(128)(2,1)}, u32[]{:S(2)}) copy-start(bf16[1024]{0:T(1024)(128)(2,1)} %param.39) | copy-start | bytes 6148
  27.7 8.6 %copy-start.13 = (bf16[1024]{0:T(1024)(128)(2,1)S(1)}, bf16[1024]{0:T(1024)(128)(2,1)}, u32[]{:S(2)}) copy-start(bf16[1024]{0:T(1024)(128)(2,1)} %param.45) | copy-start | bytes 6148
  36.3 12.2 %collective-permute-start.5 = (bf16[3072,1024]{1,0:T(8,128)(2,1)}, bf16[3072,1024]{1,0:T(8,128)(2,1)}, u32[]{:S(2)}, u32[]{:S(2)}) collective-permute-start(bf16[3072,1024]{1,0:T(8,128)(2,1)} %convolution_convert_fusion), channel_id=1, source_target_pairs={{0,1},{1,0},{2,3},{3,2},{4,5},{5,4},{6,7},{7,6},{8,9},{9,8},{10,11... | collective-permute-start | bytes 18874376 | tf_op jit(solution)/shard_map/ppermute | solution.py:629
  36.4 36.7 %collective-permute-start.1 = (bf16[3,1024]{1,0:T(4,128)(2,1)S(1)}, bf16[3,1024]{1,0:T(4,128)(2,1)S(1)}, u32[]{:S(2)}, u32[]{:S(2)}) collective-permute-start(bf16[3,1024]{1,0:T(4,128)(2,1)S(1)} %pad_maximum_fusion.17), channel_id=1, source_target_pairs={{0,2},{1,3},{2,0},{3,1},{4,6},{5,7},{6,4},{7,5},{8,10},{9,11},{10,... | collective-permute-start | bytes 18440 | tf_op jit(solution)/shard_map/ppermute | solution.py:597
  36.8 137.3 %collective-permute-start.10 = (bf16[1024,1024]{1,0:T(8,128)(2,1)}, bf16[1024,1024]{1,0:T(8,128)(2,1)}, u32[]{:S(2)}, u32[]{:S(2)}) collective-permute-start(bf16[1024,1024]{1,0:T(8,128)(2,1)} %refs_8_.1), channel_id=1, source_target_pairs={{0,1},{1,0},{2,3},{3,2},{4,5},{5,4},{6,7},{7,6},{8,9},{9,8},{10,11... | collective-permute-start | bytes 6291464 | tf_op jit(solution)/shard_map/ppermute | solution.py:591
  39.3 7.0 %copy-start.14 = (bf16[1024]{0:T(1024)(128)(2,1)S(1)}, bf16[1024]{0:T(1024)(128)(2,1)}, u32[]{:S(2)}) copy-start(bf16[1024]{0:T(1024)(128)(2,1)} %param.27) | copy-start | bytes 6148
  39.3 7.1 %copy-start.15 = (bf16[1024]{0:T(1024)(128)(2,1)S(1)}, bf16[1024]{0:T(1024)(128)(2,1)}, u32[]{:S(2)}) copy-start(bf16[1024]{0:T(1024)(128)(2,1)} %param.29) | copy-start | bytes 6148
  39.3 7.1 %copy-start.16 = (bf16[1024]{0:T(1024)(128)(2,1)S(1)}, bf16[1024]{0:T(1024)(128)(2,1)}, u32[]{:S(2)}) copy-start(bf16[1024]{0:T(1024)(128)(2,1)} %param.34) | copy-start | bytes 6148
  39.3 7.2 %copy-start.17 = (bf16[1024]{0:T(1024)(128)(2,1)S(1)}, bf16[1024]{0:T(1024)(128)(2,1)}, u32[]{:S(2)}) copy-start(bf16[1024]{0:T(1024)(128)(2,1)} %param.36) | copy-start | bytes 6148
  39.3 26.4 %collective-permute-start.11 = (bf16[512,1024]{1,0:T(8,128)(2,1)}, bf16[512,1024]{1,0:T(8,128)(2,1)}, u32[]{:S(2)}, u32[]{:S(2)}) collective-permute-start(bf16[512,1024]{1,0:T(8,128)(2,1)} %constant_dynamic-slice_fusion), channel_id=1, source_target_pairs={{0,2},{1,3},{2,0},{3,1},{4,6},{5,7},{6,4},{7,5},{8,10},{9,11},{10,... | collective-permute-start | bytes 3145736 | tf_op jit(solution)/shard_map/ppermute | solution.py:586
  46.3 22.4 %collective-permute-start.3 = (bf16[1024,1024]{1,0:T(8,128)(2,1)}, bf16[1024,1024]{1,0:T(8,128)(2,1)}, u32[]{:S(2)}, u32[]{:S(2)}) collective-permute-start(bf16[1024,1024]{1,0:T(8,128)(2,1)} %convolution_convert_fusion.1), channel_id=1, source_target_pairs={{0,1},{1,0},{2,3},{3,2},{4,5},{5,4},{6,7},{7,6},{8,9},{9,8},{10,11... | collective-permute-start | bytes 6291464 | tf_op jit(solution)/shard_map/ppermute | solution.py:629
  47.3 11.6 %slice-start = ((s8[8388608]{0:T(1024)(128)(4,1)}), s8[4194304]{0:T(1024)(128)(4,1)S(1)}, s32[]{:S(2)}) async-start(s8[8388608]{0:T(1024)(128)(4,1)} %bitcast.44), calls=%async_computation | async-start | bytes 8388608
  48.5 9.0 %copy-start.8 = (s32[1,4096]{1,0:T(1,128)S(1)}, s32[1,4096]{1,0:T(1,128)}, u32[]{:S(2)}) copy-start(s32[1,4096]{1,0:T(1,128)} %param.24) | copy-start | bytes 49156
  48.5 9.6 %copy-start.18 = (bf16[1024]{0:T(1024)(128)(2,1)S(1)}, bf16[1024]{0:T(1024)(128)(2,1)}, u32[]{:S(2)}) copy-start(bf16[1024]{0:T(1024)(128)(2,1)} %param.31) | copy-start | bytes 6148
  48.5 10.4 %slice-start.1 = ((s8[8388608]{0:T(1024)(128)(4,1)}), s8[4194304]{0:T(1024)(128)(4,1)S(1)}, s32[]{:S(2)}) async-start(s8[8388608]{0:T(1024)(128)(4,1)} %bitcast.44), calls=%async_computation.1 | async-start | bytes 8388608
  48.5 10.4 %copy-start.4 = (bf16[1024,256]{1,0:T(8,128)(2,1)S(1)}, bf16[1024,256]{1,0:T(8,128)(2,1)}, u32[]{:S(2)}) copy-start(bf16[1024,256]{1,0:T(8,128)(2,1)} %get-tuple-element.55) | copy-start | bytes 1572868
  48.5 10.4 %copy-start.5 = (bf16[1024,256]{1,0:T(8,128)(2,1)S(1)}, bf16[1024,256]{1,0:T(8,128)(2,1)}, u32[]{:S(2)}) copy-start(bf16[1024,256]{1,0:T(8,128)(2,1)} %get-tuple-element.65) | copy-start | bytes 1572868
  57.0 76.0 %collective-permute-start.6 = (bf16[3072,512]{1,0:T(8,128)(2,1)}, bf16[3072,512]{1,0:T(8,128)(2,1)S(1)}, u32[]{:S(2)}, u32[]{:S(2)}) collective-permute-start(bf16[3072,512]{1,0:T(8,128)(2,1)} %add_convert_fusion), channel_id=1, source_target_pairs={{0,2},{1,3},{2,0},{3,1},{4,6},{5,7},{6,4},{7,5},{8,10},{9,11},{10,... | collective-permute-start | bytes 9437192 | tf_op jit(solution)/shard_map/ppermute | solution.py:631
  65.7 24.1 %collective-permute-start.12 = (bf16[512,1024]{1,0:T(8,128)(2,1)}, bf16[512,1024]{1,0:T(8,128)(2,1)}, u32[]{:S(2)}, u32[]{:S(2)}) collective-permute-start(bf16[512,1024]{1,0:T(8,128)(2,1)} %collective-permute-done.11.refs_10_), channel_id=1, source_target_pairs={{0,16},{16,0},{1,17},{17,1},{2,18},{18,2},{3,19},{19,3},{4,20},{20... | collective-permute-start | bytes 3145736 | tf_op jit(solution)/shard_map/ppermute | solution.py:590
  68.7 89.6 %collective-permute-start.13 = (bf16[512,1024]{1,0:T(8,128)(2,1)}, bf16[512,1024]{1,0:T(8,128)(2,1)}, u32[]{:S(2)}, u32[]{:S(2)}) collective-permute-start(bf16[512,1024]{1,0:T(8,128)(2,1)} %collective-permute-done.11.refs_10_), channel_id=1, source_target_pairs={{0,1},{1,0},{2,3},{3,2},{4,5},{5,4},{6,7},{7,6},{8,9},{9,8},{10,11... | collective-permute-start | bytes 3145736 | tf_op jit(solution)/shard_map/ppermute | solution.py:592
  73.1 86.8 %collective-permute-start.4 = (bf16[1024,512]{1,0:T(8,128)(2,1)}, bf16[1024,512]{1,0:T(8,128)(2,1)}, u32[]{:S(2)}, u32[]{:S(2)}) collective-permute-start(bf16[1024,512]{1,0:T(8,128)(2,1)} %add_convert_fusion.1), channel_id=1, source_target_pairs={{0,2},{1,3},{2,0},{3,1},{4,6},{5,7},{6,4},{7,5},{8,10},{9,11},{10,... | collective-permute-start | bytes 3145736 | tf_op jit(solution)/shard_map/ppermute | solution.py:631
  89.9 64.4 %collective-permute-start = (bf16[3,1024]{1,0:T(4,128)(2,1)S(1)}, bf16[3,1024]{1,0:T(4,128)(2,1)S(1)}, u32[]{:S(2)}, u32[]{:S(2)}) collective-permute-start(bf16[3,1024]{1,0:T(4,128)(2,1)S(1)} %pad_maximum_fusion.17), channel_id=1, source_target_pairs={{0,1},{1,0},{2,3},{3,2},{4,5},{5,4},{6,7},{7,6},{8,9},{9,8},{10,11... | collective-permute-start | bytes 18440 | tf_op jit(solution)/shard_map/ppermute | solution.py:597
  133.1 1.7 copy-start.1
  133.1 41.0 %collective-permute-start.14 = (bf16[512,1024]{1,0:T(8,128)(2,1)}, bf16[512,1024]{1,0:T(8,128)(2,1)}, u32[]{:S(2)}, u32[]{:S(2)}) collective-permute-start(bf16[512,1024]{1,0:T(8,128)(2,1)} %collective-permute-done.12.refs_11_), channel_id=1, source_target_pairs={{0,1},{1,0},{2,3},{3,2},{4,5},{5,4},{6,7},{7,6},{8,9},{9,8},{10,11... | collective-permute-start | bytes 3145736 | tf_op jit(solution)/shard_map/ppermute | solution.py:593
  154.2 5.7 copy-start.9
  154.2 6.3 copy-start.10
  154.3 3.1 collective-permute-start.2
  157.4 16.7 %collective-permute-start.9 = (bf16[3,256,256]{2,1,0:T(8,128)(2,1)S(1)}, bf16[3,256,256]{2,1,0:T(8,128)(2,1)S(1)}, u32[]{:S(2)}, u32[]{:S(2)}) collective-permute-start(bf16[3,256,256]{2,1,0:T(8,128)(2,1)S(1)} %get-tuple-element.57), channel_id=1, source_target_pairs={{0,3},{1,2},{2,1},{3,0},{4,7},{5,6},{6,5},{7,4},{8,11},{9,10},{10,... | collective-permute-start | bytes 1179656 | tf_op jit(solution)/shard_map/ppermute | solution.py:635
  158.3 18.9 %collective-permute-start.8 = (bf16[3,256,256]{2,1,0:T(8,128)(2,1)S(1)}, bf16[3,256,256]{2,1,0:T(8,128)(2,1)S(1)}, u32[]{:S(2)}, u32[]{:S(2)}) collective-permute-start(bf16[3,256,256]{2,1,0:T(8,128)(2,1)S(1)} %get-tuple-element.58), channel_id=1, source_target_pairs={{0,2},{1,3},{2,0},{3,1},{4,6},{5,7},{6,4},{7,5},{8,10},{9,11},{10,... | collective-permute-start | bytes 1179656 | tf_op jit(solution)/shard_map/ppermute | solution.py:635
  159.9 17.3 %collective-permute-start.7 = (bf16[3,256,256]{2,1,0:T(8,128)(2,1)S(1)}, bf16[3,256,256]{2,1,0:T(8,128)(2,1)S(1)}, u32[]{:S(2)}, u32[]{:S(2)}) collective-permute-start(bf16[3,256,256]{2,1,0:T(8,128)(2,1)S(1)} %get-tuple-element.59), channel_id=1, source_target_pairs={{0,1},{1,0},{2,3},{3,2},{4,5},{5,4},{6,7},{7,6},{8,9},{9,8},{10,11... | collective-permute-start | bytes 1179656 | tf_op jit(solution)/shard_map/ppermute | solution.py:635
  174.1 3.1 copy-start.19
  177.2 0.7 copy-start.20
  177.3 0.9 copy-start.21
